TPU v7x, 32 devices: a whole 2x2x4 slice. The times are simulated.
32 devices in a mesh: seg: 4 (over y, x), tile: 8 (over z, core).
Axes of the slice: x: 2, y: 2, z: 4, core: 2. Of those that a mesh axis runs over, the one named last changes fastest.
Arguments:
- starting_warmth: float32 [256, 65536], P('tile', 'seg'), may hold values from 0 to 1
- diffusivity_field: float32 [256, 65536], P('tile', 'seg'), may hold values from 0.1 to 1
- emitter_mask: int32 [256, 65536], P('tile', 'seg'), may hold values 0 or 1
Outputs:
- final_warmth: float32 [256, 65536], P('tile', 'seg')
Inputs may be any that keep to these rules, and one draw needn't show every extreme that they name: `emitter_mask`: nonzero marks a source vertex.
All inputs are finite; a program needn't handle non-finite values. No bound on the sum of `emitter_mask` on one device may be relied on, other than what follows from the above.
Results may differ from a plain program's by a relative error of at most 0.00002.
Values sent between devices are 32-bit elements; how exact they have to be, the bound alone decides.
A program may use at most 128 MiB of HBM per device.

v0:
```python
import jax
import jax.numpy as jnp
from jax import lax
from jax.sharding import PartitionSpec as P

STEPS = 8


time_step = 0.24


def padded(shard, sides, width):
    for axis, dim in sides:
        size, length = (lax.axis_size(axis), shard.shape[dim])
        up = [(i, (i + 1) % size) for i in range(size - 1)]
        down = [(j, i) for i, j in up]
        last = lax.slice_in_dim(shard, length - width, length, axis=dim)
        first = lax.slice_in_dim(shard, 0, width, axis=dim)
        before = lax.ppermute(last, axis, up)
        after = lax.ppermute(first, axis, down)
        shard = jnp.concatenate([before, shard, after], axis=dim)
    return shard


def advance(bordered_grid, conduct, source, interior_region):
    height = bordered_grid.shape[0] - 2
    length = bordered_grid.shape[1] - 2
    middle_point = bordered_grid[1:-1, 1:-1]
    self_conductance = conduct[1:-1, 1:-1]
    flux_sum = jnp.zeros_like(middle_point)
    for row_off, col_off in ((0, 1), (2, 1), (1, 0), (1, 2)):
        adjacent_cell = bordered_grid[row_off : row_off + height, col_off : col_off + length]
        near_conduct = conduct[row_off : row_off + height, col_off : col_off + length]
        flux_sum = flux_sum + 0.5 * (self_conductance + near_conduct) * (
            adjacent_cell - middle_point
        )
    updated = middle_point + time_step * flux_sum
    updated = jnp.where(source, jnp.float32(1.0), updated)
    if interior_region is not None:
        updated = updated * interior_region
    return updated


def shards(starting_warmth, diffusivity_field, emitter_mask):
    rows_all, cols_all = starting_warmth.shape
    is_source = emitter_mask != 0
    present_warmth = starting_warmth
    stacked = jnp.stack([diffusivity_field, emitter_mask.astype(jnp.float32)])
    fixed_wide = padded(stacked, (("seg", 2), ("tile", 1)), 2)
    conduct_wide = fixed_wide[0]
    conduct_inner = conduct_wide[1:-1, 1:-1]
    source_margin = fixed_wide[1, 1:-1, 1:-1] > 0.5
    row_ids = lax.axis_index("tile") * rows_all + lax.iota(jnp.int32, rows_all + 2) - 1
    col_ids = lax.axis_index("seg") * cols_all + lax.iota(jnp.int32, cols_all + 2) - 1
    row_inside = (row_ids >= 0) & (row_ids < rows_all * lax.axis_size("tile"))
    column_interior = (col_ids >= 0) & (col_ids < cols_all * lax.axis_size("seg"))
    interior_region = (row_inside[:, None] & column_interior[None, :]).astype(jnp.float32)
    for pair_step in range(STEPS // 2):
        widened = padded(present_warmth, (("seg", 1), ("tile", 0)), 2)
        middle = advance(widened, conduct_wide, source_margin, interior_region)
        present_warmth = advance(middle, conduct_inner, is_source, None)
    return present_warmth


def solution(mesh):
    return jax.shard_map(
        shards,
        mesh=mesh,
        in_specs=(P("tile", "seg"), P("tile", "seg"), P("tile", "seg")),
        out_specs=P("tile", "seg"),
        check_vma=False,
    )
```

profile of v0, /device:TPU:5, one launch (start us, length us, event | category | flops | bytes accessed | tf_op | source)
XLA Modules:
  0.0 185.1 jit_solution(10847450932327779057)
XLA Ops:
  0.0 1.0 fusion.119
  1.0 3.1 %collective-permute-start.5 = (f32[32,2]{1,0:T(8,128)S(1)}, f32[32,2]{1,0:T(8,128)S(1)}, u32[]{:S(2)}, u32[]{:S(2)}) collective-permute-start(f32[32,2]{1,0:T(8,128)S(1)} %get-tuple-element.35), channel_id=1, source_target_pairs={{8,0},{16,8},{24,16},{9,1},{17,9},{25,17},{10,2},{18,10},{26,18},{... | collective-permute-start | bytes 776 | tf_op jit(solution)/shard_map/ppermute | solution.py:20
  4.0 2.2 %collective-permute-start.4 = (f32[32,2]{1,0:T(8,128)S(1)}, f32[32,2]{1,0:T(8,128)S(1)}, u32[]{:S(2)}, u32[]{:S(2)}) collective-permute-start(f32[32,2]{1,0:T(8,128)S(1)} %get-tuple-element.36), channel_id=1, source_target_pairs={{0,8},{8,16},{16,24},{1,9},{9,17},{17,25},{2,10},{10,18},{18,26},{... | collective-permute-start | bytes 776 | tf_op jit(solution)/shard_map/ppermute | solution.py:19
  6.2 1.7 convert_bitcast_fusion
  8.0 0.1 fusion.101
  8.1 4.0 %collective-permute-start.1 = (f32[2,32,2]{2,1,0:T(8,128)S(1)}, f32[2,32,2]{2,1,0:T(8,128)S(1)}, u32[]{:S(2)}, u32[]{:S(2)}) collective-permute-start(f32[2,32,2]{2,1,0:T(8,128)S(1)} %get-tuple-element.19), channel_id=1, source_target_pairs={{8,0},{16,8},{24,16},{9,1},{17,9},{25,17},{10,2},{18,10},{26,18},{... | collective-permute-start | bytes 1544 | tf_op jit(solution)/shard_map/ppermute | solution.py:20
  12.0 1.9 %collective-permute-start = (f32[2,32,2]{2,1,0:T(8,128)S(1)}, f32[2,32,2]{2,1,0:T(8,128)S(1)}, u32[]{:S(2)}, u32[]{:S(2)}) collective-permute-start(f32[2,32,2]{2,1,0:T(8,128)S(1)} %get-tuple-element.20), channel_id=1, source_target_pairs={{0,8},{8,16},{16,24},{1,9},{9,17},{17,25},{2,10},{10,18},{18,26},{... | collective-permute-start | bytes 1544 | tf_op jit(solution)/shard_map/ppermute | solution.py:19
  14.0 2.3 %pad_maximum_fusion = f32[2,32,16384]{2,1,0:T(8,128)} fusion(f32[1,32,16384]{2,1,0:T(8,128)S(1)} %convert_bitcast_fusion, f32[1,32,16384]{2,1,0:T(8,128)S(1)} %bitcast.9), kind=kLoop, calls=%fused_computation.2 | loop fusion | flops 1048576 | bytes 8388608 | tf_op jit(solution)/shard_map/stack | solution.py:48
  16.3 3.1 %concatenate.56 = f32[32,16388]{1,0:T(8,128)S(1)} concatenate(f32[32,2]{1,0:T(8,128)S(1)} %collective-permute-done.4, f32[32,16384]{1,0:T(8,128)} %param.3, f32[32,2]{1,0:T(8,128)S(1)} %collective-permute-done.5), dimensions={1} | concatenate | bytes 4195328 | tf_op jit(solution)/shard_map/concatenate | solution.py:21
  19.4 0.9 fusion.115
  20.3 4.6 %collective-permute-start.6 = (f32[2,16388]{1,0:T(2,128)}, f32[2,16388]{1,0:T(2,128)S(1)}, u32[]{:S(2)}, u32[]{:S(2)}) collective-permute-start(f32[2,16388]{1,0:T(2,128)} %get-tuple-element.27), channel_id=1, source_target_pairs={{0,1},{1,2},{2,3},{3,4},{4,5},{5,6},{6,7},{8,9},{9,10},{10,11},{11... | collective-permute-start | bytes 393320 | tf_op jit(solution)/shard_map/ppermute | solution.py:19
  24.9 1.9 %collective-permute-start.7 = (f32[2,16388]{1,0:T(2,128)S(1)}, f32[2,16388]{1,0:T(2,128)S(1)}, u32[]{:S(2)}, u32[]{:S(2)}) collective-permute-start(f32[2,16388]{1,0:T(2,128)S(1)} %get-tuple-element.28), channel_id=1, source_target_pairs={{1,0},{2,1},{3,2},{4,3},{5,4},{6,5},{7,6},{9,8},{10,9},{11,10},{12... | collective-permute-start | bytes 393320 | tf_op jit(solution)/shard_map/ppermute | solution.py:20
  26.8 7.3 %concatenate.54 = f32[2,32,16388]{2,1,0:T(8,128)} concatenate(f32[2,32,2]{2,1,0:T(8,128)S(1)} %collective-permute-done, f32[2,32,16384]{2,1,0:T(8,128)} %pad_maximum_fusion, f32[2,32,2]{2,1,0:T(8,128)S(1)} %collective-permute-done.1), dimensions={2} | concatenate | bytes 8390656 | tf_op jit(solution)/shard_map/concatenate | solution.py:21
  34.2 1.7 fusion.111
  35.9 3.9 %collective-permute-start.2 = (f32[2,2,16388]{2,1,0:T(2,128)S(1)}, f32[2,2,16388]{2,1,0:T(2,128)S(1)}, u32[]{:S(2)}, u32[]{:S(2)}) collective-permute-start(f32[2,2,16388]{2,1,0:T(2,128)S(1)} %get-tuple-element.17), channel_id=1, source_target_pairs={{0,1},{1,2},{2,3},{3,4},{4,5},{5,6},{6,7},{8,9},{9,10},{10,11},{11... | collective-permute-start | bytes 786632 | tf_op jit(solution)/shard_map/ppermute | solution.py:19
  39.8 1.9 %collective-permute-start.3 = (f32[2,2,16388]{2,1,0:T(2,128)S(1)}, f32[2,2,16388]{2,1,0:T(2,128)S(1)}, u32[]{:S(2)}, u32[]{:S(2)}) collective-permute-start(f32[2,2,16388]{2,1,0:T(2,128)S(1)} %get-tuple-element.18), channel_id=1, source_target_pairs={{1,0},{2,1},{3,2},{4,3},{5,4},{6,5},{7,6},{9,8},{10,9},{11,10},{12... | collective-permute-start | bytes 786632 | tf_op jit(solution)/shard_map/ppermute | solution.py:20
  41.8 0.3 pad_maximum_fusion.10
  42.1 1.0 collective-permute-done.2
  43.1 4.4 %collective-permute-done.3 = f32[2,2,16388]{2,1,0:T(2,128)S(1)} collective-permute-done((f32[2,2,16388]{2,1,0:T(2,128)S(1)}, f32[2,2,16388]{2,1,0:T(2,128)S(1)}, u32[]{:S(2)}, u32[]{:S(2)}) %collective-permute-start.3) | collective-permute-done | bytes 262240 | tf_op jit(solution)/shard_map/ppermute | solution.py:20
  47.5 0.6 pad_maximum_fusion.1
  48.2 2.3 %copy-done.6 = f32[2,36,16388]{2,1,0:T(8,128)} copy-done((f32[2,36,16388]{2,1,0:T(8,128)}, f32[2,36,16388]{2,1,0:T(8,128)S(1)}, u32[]{:S(2)}) %copy-start.6) | copy-done | bytes 4719768
  50.5 0.2 slice_bitcast_fusion
  50.7 10.8 %and_select_fusion.3 = (f32[34,16386]{1,0:T(8,128)S(1)}, f32[34,16386]{1,0:T(8,128)S(1)}, f32[34,16386]{1,0:T(8,128)}, f32[34,16386]{1,0:T(8,128)}, f32[34,16386]{1,0:T(8,128)}, /*index=5*/pred[34,16386]{1,0:T(8,128)(4,1)S(1)}) fusion(f32[36,16388]{1,0:T(8,128)S(1)} %pad_maximum_fusion.10, f32[2,16388]{1,0:T(2,128)} %copy-done.16, f32[32,16388]{1,0:T(8,128)} %copy-done.7, ...), kind=kLoop, calls=%fused_computation.9 | loop fusion | flops 15042348 | bytes 34132360 | tf_op jit(solution)/shard_map/mul | solution.py:40
  61.5 8.3 %fusion.87 = (f32[32,16384]{1,0:T(8,128)S(1)}, f32[32,16384]{1,0:T(8,128)}, f32[32,16384]{1,0:T(8,128)}, f32[32,16384]{1,0:T(8,128)}, f32[32,16384]{1,0:T(8,128)}, /*index=5*/pred[32,16384]{1,0:T(8,128)(4,1)}) fusion(f32[34,16386]{1,0:T(8,128)S(1)} %get-tuple-element.11, f32[36,16388]{1,0:T(8,128)S(1)} %slice_bitcast_fusion, s32[32,16384]{1,0:T(8,128)} %param.5), kind=kLoop, calls=%fused_computation.136 | loop fusion | flops 12058624 | bytes 34078720 | tf_op jit(solution)/shard_map/jit(_where)/select_n | solution.py:38
  69.8 1.3 copy-done.9
  71.2 0.1 fusion.118
  71.2 4.5 %collective-permute-start.9 = (f32[32,2]{1,0:T(8,128)S(1)}, f32[32,2]{1,0:T(8,128)S(1)}, u32[]{:S(2)}, u32[]{:S(2)}) collective-permute-start(f32[32,2]{1,0:T(8,128)S(1)} %get-tuple-element.33), channel_id=1, source_target_pairs={{8,0},{16,8},{24,16},{9,1},{17,9},{25,17},{10,2},{18,10},{26,18},{... | collective-permute-start | bytes 776 | tf_op jit(solution)/shard_map/ppermute | solution.py:20
  75.8 1.9 %collective-permute-start.8 = (f32[32,2]{1,0:T(8,128)S(1)}, f32[32,2]{1,0:T(8,128)S(1)}, u32[]{:S(2)}, u32[]{:S(2)}) collective-permute-start(f32[32,2]{1,0:T(8,128)S(1)} %get-tuple-element.34), channel_id=1, source_target_pairs={{0,8},{8,16},{16,24},{1,9},{9,17},{17,25},{2,10},{10,18},{18,26},{... | collective-permute-start | bytes 776 | tf_op jit(solution)/shard_map/ppermute | solution.py:19
  77.7 3.4 %collective-permute-done.8 = f32[32,2]{1,0:T(8,128)S(1)} collective-permute-done((f32[32,2]{1,0:T(8,128)S(1)}, f32[32,2]{1,0:T(8,128)S(1)}, u32[]{:S(2)}, u32[]{:S(2)}) %collective-permute-start.8) | collective-permute-done | bytes 288 | tf_op jit(solution)/shard_map/ppermute | solution.py:19
  81.2 4.2 %concatenate.60 = f32[32,16388]{1,0:T(8,128)} concatenate(f32[32,2]{1,0:T(8,128)S(1)} %collective-permute-done.8, f32[32,16384]{1,0:T(8,128)} %copy-done.9, f32[32,2]{1,0:T(8,128)S(1)} %collective-permute-done.9), dimensions={1} | concatenate | bytes 4195328 | tf_op jit(solution)/shard_map/concatenate | solution.py:21
  85.3 1.4 fusion.114
  86.8 3.3 %collective-permute-start.10 = (f32[2,16388]{1,0:T(2,128)S(1)}, f32[2,16388]{1,0:T(2,128)S(1)}, u32[]{:S(2)}, u32[]{:S(2)}) collective-permute-start(f32[2,16388]{1,0:T(2,128)S(1)} %get-tuple-element.25), channel_id=1, source_target_pairs={{0,1},{1,2},{2,3},{3,4},{4,5},{5,6},{6,7},{8,9},{9,10},{10,11},{11... | collective-permute-start | bytes 393320 | tf_op jit(solution)/shard_map/ppermute | solution.py:19
  90.1 2.1 %collective-permute-start.11 = (f32[2,16388]{1,0:T(2,128)S(1)}, f32[2,16388]{1,0:T(2,128)S(1)}, u32[]{:S(2)}, u32[]{:S(2)}) collective-permute-start(f32[2,16388]{1,0:T(2,128)S(1)} %get-tuple-element.26), channel_id=1, source_target_pairs={{1,0},{2,1},{3,2},{4,3},{5,4},{6,5},{7,6},{9,8},{10,9},{11,10},{12... | collective-permute-start | bytes 393320 | tf_op jit(solution)/shard_map/ppermute | solution.py:20
  92.2 4.2 %collective-permute-done.11 = f32[2,16388]{1,0:T(2,128)S(1)} collective-permute-done((f32[2,16388]{1,0:T(2,128)S(1)}, f32[2,16388]{1,0:T(2,128)S(1)}, u32[]{:S(2)}, u32[]{:S(2)}) %collective-permute-start.11) | collective-permute-done | bytes 131136 | tf_op jit(solution)/shard_map/ppermute | solution.py:20
  96.4 1.9 %pad_maximum_fusion.11 = f32[36,16388]{1,0:T(8,128)S(1)} fusion(f32[2,16388]{1,0:T(2,128)S(1)} %collective-permute-done.11, f32[32,16388]{1,0:T(8,128)} %concatenate.60, f32[2,16388]{1,0:T(2,128)S(1)} %collective-permute-done.10), kind=kLoop, calls=%fused_computation.85 | loop fusion | flops 1179936 | bytes 4719744 | tf_op jit(solution)/shard_map/concatenate | solution.py:21
  98.3 5.5 %and_select_fusion.2 = f32[34,16386]{1,0:T(8,128)S(1)} fusion(pred[34,16386]{1,0:T(8,128)(4,1)S(1)} %get-tuple-element.16, f32[34,16386]{1,0:T(8,128)} %get-tuple-element.15, f32[36,16388]{1,0:T(8,128)S(1)} %pad_maximum_fusion.11, f32[34,16386]{1,0:T(8,128)S(1)} %copy-done.3, f32[34,16386]{1,0:T(8,128)S(1)} %copy-done, ...), kind=kLoop, calls=%fused_computation.8 | loop fusion | flops 10028232 | bytes 20761384 | tf_op jit(solution)/shard_map/mul | solution.py:40
  103.9 5.8 %fusion.77 = f32[32,16384]{1,0:T(8,128)S(1)} fusion(pred[32,16384]{1,0:T(8,128)(4,1)S(1)} %copy-done.13, f32[32,16384]{1,0:T(8,128)} %get-tuple-element.9, f32[34,16386]{1,0:T(8,128)S(1)} %and_select_fusion.2, f32[32,16384]{1,0:T(8,128)} %get-tuple-element.8, f32[32,16384]{1,0:T(8,128)} %get-tuple-element.7, f32[32,16384]{1,0:T(8,128)} %get-tuple-element.6), kind=kLoop, calls=%fused_computation.122 | loop fusion | flops 7340032 | bytes 21495808 | tf_op jit(solution)/shard_map/jit(_where)/select_n | solution.py:38
  109.7 1.3 copy-done.10
  111.1 0.1 fusion.117
  111.1 1.9 %collective-permute-start.13 = (f32[32,2]{1,0:T(8,128)S(1)}, f32[32,2]{1,0:T(8,128)S(1)}, u32[]{:S(2)}, u32[]{:S(2)}) collective-permute-start(f32[32,2]{1,0:T(8,128)S(1)} %get-tuple-element.31), channel_id=1, source_target_pairs={{8,0},{16,8},{24,16},{9,1},{17,9},{25,17},{10,2},{18,10},{26,18},{... | collective-permute-start | bytes 776 | tf_op jit(solution)/shard_map/ppermute | solution.py:20
  113.0 3.4 %collective-permute-start.12 = (f32[32,2]{1,0:T(8,128)S(1)}, f32[32,2]{1,0:T(8,128)S(1)}, u32[]{:S(2)}, u32[]{:S(2)}) collective-permute-start(f32[32,2]{1,0:T(8,128)S(1)} %get-tuple-element.32), channel_id=1, source_target_pairs={{0,8},{8,16},{16,24},{1,9},{9,17},{17,25},{2,10},{10,18},{18,26},{... | collective-permute-start | bytes 776 | tf_op jit(solution)/shard_map/ppermute | solution.py:19
  116.4 2.0 %collective-permute-done.12 = f32[32,2]{1,0:T(8,128)S(1)} collective-permute-done((f32[32,2]{1,0:T(8,128)S(1)}, f32[32,2]{1,0:T(8,128)S(1)}, u32[]{:S(2)}, u32[]{:S(2)}) %collective-permute-start.12) | collective-permute-done | bytes 288 | tf_op jit(solution)/shard_map/ppermute | solution.py:19
  118.4 4.2 %concatenate.64 = f32[32,16388]{1,0:T(8,128)} concatenate(f32[32,2]{1,0:T(8,128)S(1)} %collective-permute-done.12, f32[32,16384]{1,0:T(8,128)} %copy-done.10, f32[32,2]{1,0:T(8,128)S(1)} %collective-permute-done.13), dimensions={1} | concatenate | bytes 4195328 | tf_op jit(solution)/shard_map/concatenate | solution.py:21
  122.6 1.4 fusion.113
  124.0 3.1 %collective-permute-start.14 = (f32[2,16388]{1,0:T(2,128)S(1)}, f32[2,16388]{1,0:T(2,128)S(1)}, u32[]{:S(2)}, u32[]{:S(2)}) collective-permute-start(f32[2,16388]{1,0:T(2,128)S(1)} %get-tuple-element.23), channel_id=1, source_target_pairs={{0,1},{1,2},{2,3},{3,4},{4,5},{5,6},{6,7},{8,9},{9,10},{10,11},{11... | collective-permute-start | bytes 393320 | tf_op jit(solution)/shard_map/ppermute | solution.py:19
  127.1 1.9 %collective-permute-start.15 = (f32[2,16388]{1,0:T(2,128)S(1)}, f32[2,16388]{1,0:T(2,128)S(1)}, u32[]{:S(2)}, u32[]{:S(2)}) collective-permute-start(f32[2,16388]{1,0:T(2,128)S(1)} %get-tuple-element.24), channel_id=1, source_target_pairs={{1,0},{2,1},{3,2},{4,3},{5,4},{6,5},{7,6},{9,8},{10,9},{11,10},{12... | collective-permute-start | bytes 393320 | tf_op jit(solution)/shard_map/ppermute | solution.py:20
  129.0 0.0 collective-permute-done.14
  129.1 4.4 %collective-permute-done.15 = f32[2,16388]{1,0:T(2,128)S(1)} collective-permute-done((f32[2,16388]{1,0:T(2,128)S(1)}, f32[2,16388]{1,0:T(2,128)S(1)}, u32[]{:S(2)}, u32[]{:S(2)}) %collective-permute-start.15) | collective-permute-done | bytes 131136 | tf_op jit(solution)/shard_map/ppermute | solution.py:20
  133.4 1.9 %pad_maximum_fusion.12 = f32[36,16388]{1,0:T(8,128)S(1)} fusion(f32[2,16388]{1,0:T(2,128)S(1)} %collective-permute-done.15, f32[32,16388]{1,0:T(8,128)} %concatenate.64, f32[2,16388]{1,0:T(2,128)S(1)} %collective-permute-done.14), kind=kLoop, calls=%fused_computation.86 | loop fusion | flops 1179936 | bytes 4719744 | tf_op jit(solution)/shard_map/concatenate | solution.py:21
  135.4 5.5 %and_select_fusion.1 = f32[34,16386]{1,0:T(8,128)S(1)} fusion(pred[34,16386]{1,0:T(8,128)(4,1)S(1)} %get-tuple-element.16, f32[34,16386]{1,0:T(8,128)} %get-tuple-element.15, f32[36,16388]{1,0:T(8,128)S(1)} %pad_maximum_fusion.12, f32[34,16386]{1,0:T(8,128)S(1)} %copy-done.4, f32[34,16386]{1,0:T(8,128)S(1)} %copy-done.1, ...), kind=kLoop, calls=%fused_computation.7 | loop fusion | flops 10028232 | bytes 20761384 | tf_op jit(solution)/shard_map/mul | solution.py:40
  140.9 5.8 %fusion.67 = f32[32,16384]{1,0:T(8,128)S(1)} fusion(pred[32,16384]{1,0:T(8,128)(4,1)S(1)} %copy-done.14, f32[32,16384]{1,0:T(8,128)} %get-tuple-element.9, f32[34,16386]{1,0:T(8,128)S(1)} %and_select_fusion.1, f32[32,16384]{1,0:T(8,128)} %get-tuple-element.8, f32[32,16384]{1,0:T(8,128)} %get-tuple-element.7, f32[32,16384]{1,0:T(8,128)} %get-tuple-element.6), kind=kLoop, calls=%fused_computation.108 | loop fusion | flops 7340032 | bytes 21495808 | tf_op jit(solution)/shard_map/jit(_where)/select_n | solution.py:38
  146.7 1.3 copy-done.11
  148.1 0.1 fusion.116
  148.1 1.9 %collective-permute-start.17 = (f32[32,2]{1,0:T(8,128)S(1)}, f32[32,2]{1,0:T(8,128)S(1)}, u32[]{:S(2)}, u32[]{:S(2)}) collective-permute-start(f32[32,2]{1,0:T(8,128)S(1)} %get-tuple-element.29), channel_id=1, source_target_pairs={{8,0},{16,8},{24,16},{9,1},{17,9},{25,17},{10,2},{18,10},{26,18},{... | collective-permute-start | bytes 776 | tf_op jit(solution)/shard_map/ppermute | solution.py:20
  150.1 3.4 %collective-permute-start.16 = (f32[32,2]{1,0:T(8,128)S(1)}, f32[32,2]{1,0:T(8,128)S(1)}, u32[]{:S(2)}, u32[]{:S(2)}) collective-permute-start(f32[32,2]{1,0:T(8,128)S(1)} %get-tuple-element.30), channel_id=1, source_target_pairs={{0,8},{8,16},{16,24},{1,9},{9,17},{17,25},{2,10},{10,18},{18,26},{... | collective-permute-start | bytes 776 | tf_op jit(solution)/shard_map/ppermute | solution.py:19
  153.4 2.0 %collective-permute-done.16 = f32[32,2]{1,0:T(8,128)S(1)} collective-permute-done((f32[32,2]{1,0:T(8,128)S(1)}, f32[32,2]{1,0:T(8,128)S(1)}, u32[]{:S(2)}, u32[]{:S(2)}) %collective-permute-start.16) | collective-permute-done | bytes 288 | tf_op jit(solution)/shard_map/ppermute | solution.py:19
  155.4 4.2 %concatenate.68 = f32[32,16388]{1,0:T(8,128)} concatenate(f32[32,2]{1,0:T(8,128)S(1)} %collective-permute-done.16, f32[32,16384]{1,0:T(8,128)} %copy-done.11, f32[32,2]{1,0:T(8,128)S(1)} %collective-permute-done.17), dimensions={1} | concatenate | bytes 4195328 | tf_op jit(solution)/shard_map/concatenate | solution.py:21
  159.6 1.4 fusion.112
  161.1 3.1 %collective-permute-start.18 = (f32[2,16388]{1,0:T(2,128)S(1)}, f32[2,16388]{1,0:T(2,128)S(1)}, u32[]{:S(2)}, u32[]{:S(2)}) collective-permute-start(f32[2,16388]{1,0:T(2,128)S(1)} %get-tuple-element.21), channel_id=1, source_target_pairs={{0,1},{1,2},{2,3},{3,4},{4,5},{5,6},{6,7},{8,9},{9,10},{10,11},{11... | collective-permute-start | bytes 393320 | tf_op jit(solution)/shard_map/ppermute | solution.py:19
  164.1 2.1 %collective-permute-start.19 = (f32[2,16388]{1,0:T(2,128)S(1)}, f32[2,16388]{1,0:T(2,128)S(1)}, u32[]{:S(2)}, u32[]{:S(2)}) collective-permute-start(f32[2,16388]{1,0:T(2,128)S(1)} %get-tuple-element.22), channel_id=1, source_target_pairs={{1,0},{2,1},{3,2},{4,3},{5,4},{6,5},{7,6},{9,8},{10,9},{11,10},{12... | collective-permute-start | bytes 393320 | tf_op jit(solution)/shard_map/ppermute | solution.py:20
  166.3 4.1 %collective-permute-done.19 = f32[2,16388]{1,0:T(2,128)S(1)} collective-permute-done((f32[2,16388]{1,0:T(2,128)S(1)}, f32[2,16388]{1,0:T(2,128)S(1)}, u32[]{:S(2)}, u32[]{:S(2)}) %collective-permute-start.19) | collective-permute-done | bytes 131136 | tf_op jit(solution)/shard_map/ppermute | solution.py:20
  170.4 1.9 %pad_maximum_fusion.13 = f32[36,16388]{1,0:T(8,128)S(1)} fusion(f32[2,16388]{1,0:T(2,128)S(1)} %collective-permute-done.19, f32[32,16388]{1,0:T(8,128)} %concatenate.68, f32[2,16388]{1,0:T(2,128)S(1)} %collective-permute-done.18), kind=kLoop, calls=%fused_computation.87 | loop fusion | flops 1179936 | bytes 4719744 | tf_op jit(solution)/shard_map/concatenate | solution.py:21
  172.4 5.5 %and_select_fusion = f32[34,16386]{1,0:T(8,128)S(1)} fusion(pred[34,16386]{1,0:T(8,128)(4,1)S(1)} %get-tuple-element.16, f32[34,16386]{1,0:T(8,128)} %get-tuple-element.15, f32[36,16388]{1,0:T(8,128)S(1)} %pad_maximum_fusion.13, f32[34,16386]{1,0:T(8,128)S(1)} %copy-done.5, f32[34,16386]{1,0:T(8,128)S(1)} %copy-done.2, ...), kind=kLoop, calls=%fused_computation.6 | loop fusion | flops 10028232 | bytes 20761384 | tf_op jit(solution)/shard_map/mul | solution.py:40
  177.9 7.2 %fusion.57 = f32[32,16384]{1,0:T(8,128)} fusion(pred[32,16384]{1,0:T(8,128)(4,1)S(1)} %copy-done.15, f32[32,16384]{1,0:T(8,128)} %get-tuple-element.9, f32[34,16386]{1,0:T(8,128)S(1)} %and_select_fusion, f32[32,16384]{1,0:T(8,128)} %get-tuple-element.8, f32[32,16384]{1,0:T(8,128)} %get-tuple-element.7, f32[32,16384]{1,0:T(8,128)} %get-tuple-element.6), kind=kLoop, calls=%fused_computation.94 | loop fusion | flops 7340032 | bytes 21495808 | tf_op jit(solution)/shard_map/jit(_where)/select_n | solution.py:38
  (43 shorter events, 0.1 us)
Async XLA Ops:
  0.0 8.0 %copy-start.12 = (f32[32,16384]{1,0:T(8,128)S(1)}, f32[32,16384]{1,0:T(8,128)}, u32[]{:S(2)}) copy-start(f32[32,16384]{1,0:T(8,128)} %param.4) | copy-start | bytes 6291460
  1.0 15.3 %collective-permute-start.5 = (f32[32,2]{1,0:T(8,128)S(1)}, f32[32,2]{1,0:T(8,128)S(1)}, u32[]{:S(2)}, u32[]{:S(2)}) collective-permute-start(f32[32,2]{1,0:T(8,128)S(1)} %get-tuple-element.35), channel_id=1, source_target_pairs={{8,0},{16,8},{24,16},{9,1},{17,9},{25,17},{10,2},{18,10},{26,18},{... | collective-permute-start | bytes 776 | tf_op jit(solution)/shard_map/ppermute | solution.py:20
  4.0 12.3 %collective-permute-start.4 = (f32[32,2]{1,0:T(8,128)S(1)}, f32[32,2]{1,0:T(8,128)S(1)}, u32[]{:S(2)}, u32[]{:S(2)}) collective-permute-start(f32[32,2]{1,0:T(8,128)S(1)} %get-tuple-element.36), channel_id=1, source_target_pairs={{0,8},{8,16},{16,24},{1,9},{9,17},{17,25},{2,10},{10,18},{18,26},{... | collective-permute-start | bytes 776 | tf_op jit(solution)/shard_map/ppermute | solution.py:19
  8.1 18.8 %collective-permute-start.1 = (f32[2,32,2]{2,1,0:T(8,128)S(1)}, f32[2,32,2]{2,1,0:T(8,128)S(1)}, u32[]{:S(2)}, u32[]{:S(2)}) collective-permute-start(f32[2,32,2]{2,1,0:T(8,128)S(1)} %get-tuple-element.19), channel_id=1, source_target_pairs={{8,0},{16,8},{24,16},{9,1},{17,9},{25,17},{10,2},{18,10},{26,18},{... | collective-permute-start | bytes 1544 | tf_op jit(solution)/shard_map/ppermute | solution.py:20
  12.0 14.8 %collective-permute-start = (f32[2,32,2]{2,1,0:T(8,128)S(1)}, f32[2,32,2]{2,1,0:T(8,128)S(1)}, u32[]{:S(2)}, u32[]{:S(2)}) collective-permute-start(f32[2,32,2]{2,1,0:T(8,128)S(1)} %get-tuple-element.20), channel_id=1, source_target_pairs={{0,8},{8,16},{16,24},{1,9},{9,17},{17,25},{2,10},{10,18},{18,26},{... | collective-permute-start | bytes 1544 | tf_op jit(solution)/shard_map/ppermute | solution.py:19
  19.4 22.4 %copy-start.7 = (f32[32,16388]{1,0:T(8,128)}, f32[32,16388]{1,0:T(8,128)S(1)}, u32[]{:S(2)}) copy-start(f32[32,16388]{1,0:T(8,128)S(1)} %concatenate.56) | copy-start | bytes 6292996
  20.3 21.5 %collective-permute-start.6 = (f32[2,16388]{1,0:T(2,128)}, f32[2,16388]{1,0:T(2,128)S(1)}, u32[]{:S(2)}, u32[]{:S(2)}) collective-permute-start(f32[2,16388]{1,0:T(2,128)} %get-tuple-element.27), channel_id=1, source_target_pairs={{0,1},{1,2},{2,3},{3,4},{4,5},{5,6},{6,7},{8,9},{9,10},{10,11},{11... | collective-permute-start | bytes 393320 | tf_op jit(solution)/shard_map/ppermute | solution.py:19
  24.9 16.9 %collective-permute-start.7 = (f32[2,16388]{1,0:T(2,128)S(1)}, f32[2,16388]{1,0:T(2,128)S(1)}, u32[]{:S(2)}, u32[]{:S(2)}) collective-permute-start(f32[2,16388]{1,0:T(2,128)S(1)} %get-tuple-element.28), channel_id=1, source_target_pairs={{1,0},{2,1},{3,2},{4,3},{5,4},{6,5},{7,6},{9,8},{10,9},{11,10},{12... | collective-permute-start | bytes 393320 | tf_op jit(solution)/shard_map/ppermute | solution.py:20
  35.9 11.6 %copy-start.8 = (f32[2,32,16388]{2,1,0:T(8,128)S(1)}, f32[2,32,16388]{2,1,0:T(8,128)}, u32[]{:S(2)}) copy-start(f32[2,32,16388]{2,1,0:T(8,128)} %concatenate.54) | copy-start | bytes 12585988
  35.9 7.2 %collective-permute-start.2 = (f32[2,2,16388]{2,1,0:T(2,128)S(1)}, f32[2,2,16388]{2,1,0:T(2,128)S(1)}, u32[]{:S(2)}, u32[]{:S(2)}) collective-permute-start(f32[2,2,16388]{2,1,0:T(2,128)S(1)} %get-tuple-element.17), channel_id=1, source_target_pairs={{0,1},{1,2},{2,3},{3,4},{4,5},{5,6},{6,7},{8,9},{9,10},{10,11},{11... | collective-permute-start | bytes 786632 | tf_op jit(solution)/shard_map/ppermute | solution.py:19
  39.8 7.7 %collective-permute-start.3 = (f32[2,2,16388]{2,1,0:T(2,128)S(1)}, f32[2,2,16388]{2,1,0:T(2,128)S(1)}, u32[]{:S(2)}, u32[]{:S(2)}) collective-permute-start(f32[2,2,16388]{2,1,0:T(2,128)S(1)} %get-tuple-element.18), channel_id=1, source_target_pairs={{1,0},{2,1},{3,2},{4,3},{5,4},{6,5},{7,6},{9,8},{10,9},{11,10},{12... | collective-permute-start | bytes 786632 | tf_op jit(solution)/shard_map/ppermute | solution.py:20
  41.8 6.3 %copy-start.16 = (f32[2,16388]{1,0:T(2,128)}, f32[2,16388]{1,0:T(2,128)S(1)}, u32[]{:S(2)}) copy-start(f32[2,16388]{1,0:T(2,128)S(1)} %collective-permute-done.7) | copy-start | bytes 393316
  48.1 2.3 %copy-start.6 = (f32[2,36,16388]{2,1,0:T(8,128)}, f32[2,36,16388]{2,1,0:T(8,128)S(1)}, u32[]{:S(2)}) copy-start(f32[2,36,16388]{2,1,0:T(8,128)S(1)} %pad_maximum_fusion.1) | copy-start | bytes 14159236
  69.8 1.3 copy-start.9
  71.2 6.5 %collective-permute-start.9 = (f32[32,2]{1,0:T(8,128)S(1)}, f32[32,2]{1,0:T(8,128)S(1)}, u32[]{:S(2)}, u32[]{:S(2)}) collective-permute-start(f32[32,2]{1,0:T(8,128)S(1)} %get-tuple-element.33), channel_id=1, source_target_pairs={{8,0},{16,8},{24,16},{9,1},{17,9},{25,17},{10,2},{18,10},{26,18},{... | collective-permute-start | bytes 776 | tf_op jit(solution)/shard_map/ppermute | solution.py:20
  75.8 5.4 %collective-permute-start.8 = (f32[32,2]{1,0:T(8,128)S(1)}, f32[32,2]{1,0:T(8,128)S(1)}, u32[]{:S(2)}, u32[]{:S(2)}) collective-permute-start(f32[32,2]{1,0:T(8,128)S(1)} %get-tuple-element.34), channel_id=1, source_target_pairs={{0,8},{8,16},{16,24},{1,9},{9,17},{17,25},{2,10},{10,18},{18,26},{... | collective-permute-start | bytes 776 | tf_op jit(solution)/shard_map/ppermute | solution.py:19
  85.3 13.0 %copy-start.3 = (f32[34,16386]{1,0:T(8,128)S(1)}, f32[34,16386]{1,0:T(8,128)}, u32[]{:S(2)}) copy-start(f32[34,16386]{1,0:T(8,128)} %get-tuple-element.14) | copy-start | bytes 6685492
  86.8 11.5 %copy-start = (f32[34,16386]{1,0:T(8,128)S(1)}, f32[34,16386]{1,0:T(8,128)}, u32[]{:S(2)}) copy-start(f32[34,16386]{1,0:T(8,128)} %get-tuple-element.13) | copy-start | bytes 6685492
  86.8 5.4 %collective-permute-start.10 = (f32[2,16388]{1,0:T(2,128)S(1)}, f32[2,16388]{1,0:T(2,128)S(1)}, u32[]{:S(2)}, u32[]{:S(2)}) collective-permute-start(f32[2,16388]{1,0:T(2,128)S(1)} %get-tuple-element.25), channel_id=1, source_target_pairs={{0,1},{1,2},{2,3},{3,4},{4,5},{5,6},{6,7},{8,9},{9,10},{10,11},{11... | collective-permute-start | bytes 393320 | tf_op jit(solution)/shard_map/ppermute | solution.py:19
  90.1 6.3 %collective-permute-start.11 = (f32[2,16388]{1,0:T(2,128)S(1)}, f32[2,16388]{1,0:T(2,128)S(1)}, u32[]{:S(2)}, u32[]{:S(2)}) collective-permute-start(f32[2,16388]{1,0:T(2,128)S(1)} %get-tuple-element.26), channel_id=1, source_target_pairs={{1,0},{2,1},{3,2},{4,3},{5,4},{6,5},{7,6},{9,8},{10,9},{11,10},{12... | collective-permute-start | bytes 393320 | tf_op jit(solution)/shard_map/ppermute | solution.py:20
  98.3 5.5 %copy-start.13 = (pred[32,16384]{1,0:T(8,128)(4,1)S(1)}, pred[32,16384]{1,0:T(8,128)(4,1)}, u32[]{:S(2)}) copy-start(pred[32,16384]{1,0:T(8,128)(4,1)} %get-tuple-element.10) | copy-start | bytes 1572868
  109.7 1.3 copy-start.10
  111.1 5.3 %collective-permute-start.13 = (f32[32,2]{1,0:T(8,128)S(1)}, f32[32,2]{1,0:T(8,128)S(1)}, u32[]{:S(2)}, u32[]{:S(2)}) collective-permute-start(f32[32,2]{1,0:T(8,128)S(1)} %get-tuple-element.31), channel_id=1, source_target_pairs={{8,0},{16,8},{24,16},{9,1},{17,9},{25,17},{10,2},{18,10},{26,18},{... | collective-permute-start | bytes 776 | tf_op jit(solution)/shard_map/ppermute | solution.py:20
  113.0 5.4 %collective-permute-start.12 = (f32[32,2]{1,0:T(8,128)S(1)}, f32[32,2]{1,0:T(8,128)S(1)}, u32[]{:S(2)}, u32[]{:S(2)}) collective-permute-start(f32[32,2]{1,0:T(8,128)S(1)} %get-tuple-element.32), channel_id=1, source_target_pairs={{0,8},{8,16},{16,24},{1,9},{9,17},{17,25},{2,10},{10,18},{18,26},{... | collective-permute-start | bytes 776 | tf_op jit(solution)/shard_map/ppermute | solution.py:19
  122.6 12.7 %copy-start.4 = (f32[34,16386]{1,0:T(8,128)S(1)}, f32[34,16386]{1,0:T(8,128)}, u32[]{:S(2)}) copy-start(f32[34,16386]{1,0:T(8,128)} %get-tuple-element.14) | copy-start | bytes 6685492
  124.0 11.3 %copy-start.1 = (f32[34,16386]{1,0:T(8,128)S(1)}, f32[34,16386]{1,0:T(8,128)}, u32[]{:S(2)}) copy-start(f32[34,16386]{1,0:T(8,128)} %get-tuple-element.13) | copy-start | bytes 6685492
  124.0 5.0 %collective-permute-start.14 = (f32[2,16388]{1,0:T(2,128)S(1)}, f32[2,16388]{1,0:T(2,128)S(1)}, u32[]{:S(2)}, u32[]{:S(2)}) collective-permute-start(f32[2,16388]{1,0:T(2,128)S(1)} %get-tuple-element.23), channel_id=1, source_target_pairs={{0,1},{1,2},{2,3},{3,4},{4,5},{5,6},{6,7},{8,9},{9,10},{10,11},{11... | collective-permute-start | bytes 393320 | tf_op jit(solution)/shard_map/ppermute | solution.py:19
  127.1 6.3 %collective-permute-start.15 = (f32[2,16388]{1,0:T(2,128)S(1)}, f32[2,16388]{1,0:T(2,128)S(1)}, u32[]{:S(2)}, u32[]{:S(2)}) collective-permute-start(f32[2,16388]{1,0:T(2,128)S(1)} %get-tuple-element.24), channel_id=1, source_target_pairs={{1,0},{2,1},{3,2},{4,3},{5,4},{6,5},{7,6},{9,8},{10,9},{11,10},{12... | collective-permute-start | bytes 393320 | tf_op jit(solution)/shard_map/ppermute | solution.py:20
  135.3 5.5 %copy-start.14 = (pred[32,16384]{1,0:T(8,128)(4,1)S(1)}, pred[32,16384]{1,0:T(8,128)(4,1)}, u32[]{:S(2)}) copy-start(pred[32,16384]{1,0:T(8,128)(4,1)} %get-tuple-element.10) | copy-start | bytes 1572868
  146.7 1.3 copy-start.11
  148.1 5.3 %collective-permute-start.17 = (f32[32,2]{1,0:T(8,128)S(1)}, f32[32,2]{1,0:T(8,128)S(1)}, u32[]{:S(2)}, u32[]{:S(2)}) collective-permute-start(f32[32,2]{1,0:T(8,128)S(1)} %get-tuple-element.29), channel_id=1, source_target_pairs={{8,0},{16,8},{24,16},{9,1},{17,9},{25,17},{10,2},{18,10},{26,18},{... | collective-permute-start | bytes 776 | tf_op jit(solution)/shard_map/ppermute | solution.py:20
  150.1 5.4 %collective-permute-start.16 = (f32[32,2]{1,0:T(8,128)S(1)}, f32[32,2]{1,0:T(8,128)S(1)}, u32[]{:S(2)}, u32[]{:S(2)}) collective-permute-start(f32[32,2]{1,0:T(8,128)S(1)} %get-tuple-element.30), channel_id=1, source_target_pairs={{0,8},{8,16},{16,24},{1,9},{9,17},{17,25},{2,10},{10,18},{18,26},{... | collective-permute-start | bytes 776 | tf_op jit(solution)/shard_map/ppermute | solution.py:19
  159.6 12.7 %copy-start.5 = (f32[34,16386]{1,0:T(8,128)S(1)}, f32[34,16386]{1,0:T(8,128)}, u32[]{:S(2)}) copy-start(f32[34,16386]{1,0:T(8,128)} %get-tuple-element.14) | copy-start | bytes 6685492
  161.1 11.3 %copy-start.2 = (f32[34,16386]{1,0:T(8,128)S(1)}, f32[34,16386]{1,0:T(8,128)}, u32[]{:S(2)}) copy-start(f32[34,16386]{1,0:T(8,128)} %get-tuple-element.13) | copy-start | bytes 6685492
  161.1 5.2 %collective-permute-start.18 = (f32[2,16388]{1,0:T(2,128)S(1)}, f32[2,16388]{1,0:T(2,128)S(1)}, u32[]{:S(2)}, u32[]{:S(2)}) collective-permute-start(f32[2,16388]{1,0:T(2,128)S(1)} %get-tuple-element.21), channel_id=1, source_target_pairs={{0,1},{1,2},{2,3},{3,4},{4,5},{5,6},{6,7},{8,9},{9,10},{10,11},{11... | collective-permute-start | bytes 393320 | tf_op jit(solution)/shard_map/ppermute | solution.py:19
  164.1 6.3 %collective-permute-start.19 = (f32[2,16388]{1,0:T(2,128)S(1)}, f32[2,16388]{1,0:T(2,128)S(1)}, u32[]{:S(2)}, u32[]{:S(2)}) collective-permute-start(f32[2,16388]{1,0:T(2,128)S(1)} %get-tuple-element.22), channel_id=1, source_target_pairs={{1,0},{2,1},{3,2},{4,3},{5,4},{6,5},{7,6},{9,8},{10,9},{11,10},{12... | collective-permute-start | bytes 393320 | tf_op jit(solution)/shard_map/ppermute | solution.py:20
  172.4 5.5 %copy-start.15 = (pred[32,16384]{1,0:T(8,128)(4,1)S(1)}, pred[32,16384]{1,0:T(8,128)(4,1)}, u32[]{:S(2)}) copy-start(pred[32,16384]{1,0:T(8,128)(4,1)} %get-tuple-element.10) | copy-start | bytes 1572868
where the time goes:
time: 186 us; the launch traced here: 185 us
  other arithmetic  65.3 us (35%)
  starting transfers between devices  56.1 us (30%)
  local copies, waits for them, and re-layouts  37.6 us (20%)
  waiting for transfers between devices  25.6 us (14%)
    ppermute x10, starting transfers between devices, padded(): before = lax.ppermute(last, axis, up)  30.7 us
    mul x4, other arithmetic, advance(): updated = updated * interior_region  27.4 us
    select_n x4, other arithmetic, advance(): updated = jnp.where(source, jnp.float32(1.0), updated)  27.2 us
    ppermute x10, starting transfers between devices, padded(): after = lax.ppermute(first, axis, down)  25.4 us
    concatenate x5, local copies, waits for them, and re-layouts, padded(): shard = jnp.concatenate([before, shard, after], axis=dim)  22.9 us
    ppermute x10, waiting for transfers between devices, padded(): after = lax.ppermute(first, axis, down)  17.1 us
    ppermute x10, waiting for transfers between devices, padded(): before = lax.ppermute(last, axis, up)  8.49 us
    slice x5, local copies, waits for them, and re-layouts, padded(): last = lax.slice_in_dim(shard, length - width, length, axis=dim)  6.99 us
  transfers between devices with their start and end apart: 20, of which 8 were waited for; matrix products, arithmetic and copies ran while one was open for 9% of the time, Pallas kernels for 0%

commit v1 on v0

v1 whole, which is shorter than its diff:
```python
import functools

import jax
import jax.numpy as jnp
from jax import lax
from jax.experimental import pallas as pl
from jax.experimental.pallas import tpu as pltpu
from jax.sharding import PartitionSpec as P

STEPS = 8
ROUNDS = (4, 4)
DEEP = max(ROUNDS)
STEP_SIZE = 0.24
LANES = 128
SUB = 8
MESH = pl.DeviceIdType.MESH


def kernel(
    sizes, u_hbm, k_hbm, s_hbm, out_hbm,
    u_nat, k_nat, s_nat, o_nat,
    u_0, u_a, u_b, k_row, s_row, c_e, c_w, c_n, c_s, c_0,
    col_out, col_in, corner_in, row_out, row_in,
    load_sem, store_sem, col_sems, corner_sems, first_sems, row_sems,
):
    rows, blocks, n_seg, n_tile = sizes
    groups = rows // SUB
    tiles = blocks // SUB
    seg, tile = lax.axis_index("seg"), lax.axis_index("tile")
    lane = lax.broadcasted_iota(jnp.int32, (SUB, LANES), 1)
    sublane = lax.broadcasted_iota(jnp.int32, (SUB, LANES), 0)
    first_lane, last_lane = lane == 0, lane == LANES - 1
    has_side = (seg > 0, seg < n_seg - 1)
    has_row = (tile > 0, tile < n_tile - 1)
    side_step = (-1, 1)
    left_at, right_at = SUB - 1, SUB + blocks
    halo_at = (left_at, right_at)
    edge_at = (SUB, SUB + blocks - 1)

    def both(a, b):
        return jnp.logical_and(a, b)

    barrier = pltpu.get_barrier_semaphore()
    count = jnp.int32(0)
    for ds in (-1, 0, 1):
        for dt in (-1, 0, 1):
            if ds == 0 and dt == 0:
                continue
            there = jnp.bool_(True)
            if ds:
                there = has_side[(ds + 1) // 2]
            if dt:
                there = both(there, has_row[(dt + 1) // 2])
            count = count + there.astype(jnp.int32)

            @pl.when(there)
            def _(ds=ds, dt=dt):
                pl.semaphore_signal(barrier, inc=1, device_id=(seg + ds, tile + dt), device_id_type=MESH)

    span = blocks * SUB
    sources = ((u_hbm, u_nat), (k_hbm, k_nat), (s_hbm, s_nat))
    order = [0, groups - 1] + list(range(1, groups - 1))

    def load(which, g):
        src, dst = sources[which]
        part = pl.ds(g * span, span)
        return pltpu.make_async_copy(src.at[part], dst.at[part], load_sem.at[which, g])

    for g in order:
        for which in range(3):
            load(which, g).start()

    zero_plane = jnp.zeros((SUB, LANES), jnp.float32)
    for side in range(2):
        top = 0 if side == 0 else DEEP + rows

        @pl.when(jnp.logical_not(has_row[side]))
        def _(top=top):
            def clear(j, c):
                at = pl.ds(j * SUB, SUB)
                for d in range(DEEP):
                    for ref in (u_0, k_row, s_row):
                        ref[top + d, at, :] = zero_plane
                return c

            lax.fori_loop(0, tiles + 2, clear, 0)

        @pl.when(jnp.logical_not(has_side[side]))
        def _(side=side):
            for r in range(rows + 2 * DEEP):
                for ref in (u_0, k_row, s_row):
                    ref[r, halo_at[side]:halo_at[side] + 1, :] = zero_plane[:1]

    def relayout(g):
        for which in range(3):
            load(which, g).wait()

        def body(j, c):
            for r in range(SUB):
                start = g * span + j * SUB * SUB + r
                at = pl.ds(SUB + j * SUB, SUB)
                row = DEEP + g * SUB + r
                u_0[row, at, :] = u_nat[pl.ds(start, SUB, stride=SUB), :]
                k_row[row, at, :] = k_nat[pl.ds(start, SUB, stride=SUB), :]
                s_row[row, at, :] = jnp.where(
                    s_nat[pl.ds(start, SUB, stride=SUB), :] != 0, jnp.float32(1.0), jnp.float32(0.0)
                )
            return c

        lax.fori_loop(0, tiles, body, 0)

    own = pl.ds(SUB, blocks)

    def first_copy(which, side):
        ref, deep = ((u_0, ROUNDS[0]), (k_row, DEEP), (s_row, DEEP))[which]
        if side == 0:
            src, dst = pl.ds(DEEP, deep), pl.ds(DEEP + rows, deep)
        else:
            src, dst = pl.ds(DEEP + rows - deep, deep), pl.ds(DEEP - deep, deep)
        return pltpu.make_async_remote_copy(
            src_ref=ref.at[src, own], dst_ref=ref.at[dst, own],
            send_sem=first_sems.at[0, which, side], recv_sem=first_sems.at[1, which, 1 - side],
            device_id=(seg, tile + side_step[side]), device_id_type=MESH,
        )

    def first_arrival(which, side):
        ref, deep = ((u_0, ROUNDS[0]), (k_row, DEEP), (s_row, DEEP))[which]
        dst = pl.ds(DEEP - deep, deep) if side == 0 else pl.ds(DEEP + rows, deep)
        return pltpu.make_async_remote_copy(
            src_ref=ref.at[dst, own], dst_ref=ref.at[dst, own],
            send_sem=first_sems.at[0, which, side], recv_sem=first_sems.at[1, which, side],
            device_id=(seg, tile + side_step[side]), device_id_type=MESH,
        )

    relayout(0)
    relayout(groups - 1)
    pl.semaphore_wait(barrier, count)
    for side in range(2):
        @pl.when(has_row[side])
        def _(side=side):
            for which in range(3):
                first_copy(which, side).start()

    def col_copy(side):
        return pltpu.make_async_remote_copy(
            src_ref=col_out.at[side], dst_ref=col_in.at[1 - side],
            send_sem=col_sems.at[0, side], recv_sem=col_sems.at[1, 1 - side],
            device_id=(seg + side_step[side], tile), device_id_type=MESH,
        )

    def corner_copy(side, vert):
        return pltpu.make_async_remote_copy(
            src_ref=col_out.at[side, 0 if vert == 0 else groups - 1],
            dst_ref=corner_in.at[1 - side, 1 - vert],
            send_sem=corner_sems.at[0, side, vert], recv_sem=corner_sems.at[1, 1 - side, 1 - vert],
            device_id=(seg + side_step[side], tile + side_step[vert]), device_id_type=MESH,
        )

    for g in range(1, groups - 1):
        relayout(g)
    row_refs = (u_0, k_row, s_row)
    for side in range(2):
        at = edge_at[side]
        for g in range(groups):
            for which, ref in enumerate(row_refs):
                for r in range(SUB):
                    col_out[side, g, which * SUB + r:which * SUB + r + 1, :] = ref[DEEP + g * SUB + r, at:at + 1, :]

        @pl.when(has_side[side])
        def _(side=side):
            col_copy(side).start()

        for vert in range(2):
            @pl.when(both(has_side[side], has_row[vert]))
            def _(side=side, vert=vert):
                corner_copy(side, vert).start()

    for side in range(2):
        @pl.when(has_side[side])
        def _(side=side):
            col_copy(1 - side).wait_recv()
            at = halo_at[side]
            for g in range(groups):
                for which, ref in enumerate(row_refs):
                    for r in range(SUB):
                        ref[DEEP + g * SUB + r, at:at + 1, :] = col_in[side, g, which * SUB + r:which * SUB + r + 1, :]

    def east(ref, row, base, here):
        beyond = ref[row, pl.ds(base + 1, SUB), :]
        return pltpu.roll(jnp.where(first_lane, beyond, here), LANES - 1, 1)

    def west(ref, row, base, here):
        beyond = ref[row, pl.ds(base - 1, SUB), :]
        return pltpu.roll(jnp.where(last_lane, beyond, here), 1, 1)

    half = jnp.float32(0.5 * STEP_SIZE)

    def prepare(lo, hi):
        def body(g, c):
            base = g * SUB + left_at
            at = pl.ds(base, SUB)
            column = seg * blocks + base - SUB + sublane
            inside_col = jnp.logical_and(column >= 0, column < n_seg * blocks)
            above, here = k_row[DEEP + lo - 1, at, :], k_row[DEEP + lo, at, :]
            for r in range(lo, hi):
                below = k_row[DEEP + r + 1, at, :]
                live = jnp.logical_and(inside_col, s_row[DEEP + r, at, :] == 0.0)
                if r < 0:
                    live = jnp.logical_and(live, has_row[0])
                if r >= rows:
                    live = jnp.logical_and(live, has_row[1])
                weight = jnp.where(live, half, jnp.float32(0.0))
                ce = weight * (here + east(k_row, DEEP + r, base, here))
                cw = weight * (here + west(k_row, DEEP + r, base, here))
                cn = weight * (here + above)
                cs = weight * (here + below)
                c_e[DEEP + r, at, :] = ce
                c_w[DEEP + r, at, :] = cw
                c_n[DEEP + r, at, :] = cn
                c_s[DEEP + r, at, :] = cs
                c_0[DEEP + r, at, :] = 1.0 - ((ce + cw) + (cn + cs))
                above, here = here, below
            return c

        lax.fori_loop(0, tiles + 1, body, 0)

    def advance(step, lo, hi):
        src, dst = (u_b, u_a) if step % 2 == 0 else (u_a, u_b)
        src = u_0 if step == 0 else src
        last = step == STEPS - 1

        def body(g, c):
            base = g * SUB + (SUB if last else left_at)
            at = pl.ds(base, SUB)
            above, here = src[DEEP + lo - 1, at, :], src[DEEP + lo, at, :]
            for r in range(lo, hi):
                below = src[DEEP + r + 1, at, :]
                row = DEEP + r
                new = (
                    (c_0[row, at, :] * here + c_n[row, at, :] * above)
                    + (c_s[row, at, :] * below + c_e[row, at, :] * east(src, row, base, here))
                    + c_w[row, at, :] * west(src, row, base, here)
                )
                if step == 0:
                    new = jnp.where(s_row[row, at, :] != 0.0, jnp.float32(1.0), new)
                if last:
                    start = (r // SUB) * span + g * SUB * SUB + r % SUB
                    o_nat[pl.ds(start, SUB, stride=SUB), :] = new
                else:
                    dst[row, at, :] = new
                above, here = here, below
            return c

        lax.fori_loop(0, tiles if last else tiles + 1, body, 0)

    def row_copy(which, side):
        d = ROUNDS[which]
        return pltpu.make_async_remote_copy(
            src_ref=row_out.at[which, side, pl.ds(0, d)], dst_ref=row_in.at[which, 1 - side, pl.ds(0, d)],
            send_sem=row_sems.at[0, which, side], recv_sem=row_sems.at[1, which, 1 - side],
            device_id=(seg, tile + side_step[side]), device_id_type=MESH,
        )

    def move_rows(src, src_row, dst, dst_row, d):
        def body(j, c):
            at = pl.ds(j * SUB, SUB)
            for i in range(d):
                dst[dst_row + i, at, :] = src[src_row + i, at, :]
            return c

        lax.fori_loop(0, tiles + 2, body, 0)

    def store(g):
        part = pl.ds(g * span, span)
        return pltpu.make_async_copy(o_nat.at[part], out_hbm.at[part], store_sem.at[g])

    done = 0
    prepare(1, rows - 1)
    for which, d in enumerate(ROUNDS):
        if which:
            cur = u_a if done % 2 == 1 else u_b
            for side in range(2):
                move_rows(cur, DEEP if side == 0 else DEEP + rows - d, row_out.at[which, side], 0, d)

                @pl.when(has_row[side])
                def _(which=which, side=side):
                    row_copy(which, side).start()

        for j in range(1, d + 1):
            advance(done + j - 1, j, rows - j)
        if which == len(ROUNDS) - 1:
            for g in range(1, groups - 1):
                if g * SUB >= d and (g + 1) * SUB <= rows - d:
                    store(g).start()

        if which == 0:
            for side in range(2):
                @pl.when(has_row[side])
                def _(side=side):
                    for w in range(3):
                        first_arrival(w, side).wait_recv()
                        first_copy(w, side).wait_send()

            for side in range(2):
                for vert in range(2):
                    corner = both(has_side[side], has_row[vert])
                    at = halo_at[side]

                    @pl.when(corner)
                    def _(side=side, vert=vert, at=at):
                        corner_copy(1 - side, 1 - vert).wait_recv()
                        for w, ref in enumerate(row_refs):
                            for i in range(DEEP):
                                from_row = w * SUB + (SUB - DEEP + i if vert == 0 else i)
                                to_row = i if vert == 0 else DEEP + rows + i
                                ref[to_row, at:at + 1, :] = corner_in[side, vert, from_row:from_row + 1, :]
            prepare(1 - DEEP, 1)
            prepare(rows - 1, rows + DEEP - 1)
        else:
            for side in range(2):
                top = DEEP - d if side == 0 else DEEP + rows

                @pl.when(has_row[side])
                def _(which=which, side=side, top=top, cur=cur, d=d):
                    row_copy(which, 1 - side).wait_recv()
                    move_rows(row_in.at[which, side], 0, cur, top, d)

                @pl.when(jnp.logical_not(has_row[side]))
                def _(top=top, cur=cur, d=d):
                    def clear(j, c):
                        for i in range(d):
                            cur[top + i, pl.ds(j * SUB, SUB), :] = zero_plane
                        return c

                    lax.fori_loop(0, tiles + 2, clear, 0)

        for j in range(1, d + 1):
            final = done + j == STEPS
            advance(done + j - 1, 0 if final else j - d, j)
            advance(done + j - 1, rows - j, rows if final else rows - j + d)
        done += d

    for g in range(groups):
        if not (g * SUB >= d and (g + 1) * SUB <= rows - d):
            store(g).start()
    for side in range(2):
        @pl.when(has_side[side])
        def _(side=side):
            col_copy(side).wait_send()

        for vert in range(2):
            @pl.when(both(has_side[side], has_row[vert]))
            def _(side=side, vert=vert):
                corner_copy(side, vert).wait_send()

        @pl.when(has_row[side])
        def _(side=side):
            for which in range(1, len(ROUNDS)):
                row_copy(which, side).wait_send()
    for g in range(groups):
        store(g).wait()


def shards(n_seg, n_tile, warmth, conductivity, sources):
    rows, columns = warmth.shape
    blocks = columns // LANES
    groups = rows // SUB

    def planes(a):
        return a.reshape(groups, SUB, blocks, LANES).transpose(0, 2, 1, 3).reshape(-1, LANES)

    flat = rows * blocks
    f32 = jnp.float32
    plane = (rows + 2 * DEEP, blocks + 2 * SUB, LANES)
    vmem = pltpu.VMEM
    sem = pltpu.SemaphoreType.DMA
    n = len(ROUNDS)
    out = pl.pallas_call(
        functools.partial(kernel, (rows, blocks, n_seg, n_tile)),
        out_shape=jax.ShapeDtypeStruct((flat, LANES), f32),
        in_specs=[pl.BlockSpec(memory_space=pl.ANY)] * 3,
        out_specs=pl.BlockSpec(memory_space=pl.ANY),
        scratch_shapes=[
            vmem((flat, LANES), f32), vmem((flat, LANES), f32), vmem((flat, LANES), sources.dtype), vmem((flat, LANES), f32),
        ] + [vmem(plane, f32)] * 10 + [
            vmem((2, groups, 3 * SUB, LANES), f32), vmem((2, groups, 3 * SUB, LANES), f32),
            vmem((2, 2, 3 * SUB, LANES), f32),
            vmem((n, 2, DEEP, blocks + 2 * SUB, LANES), f32), vmem((n, 2, DEEP, blocks + 2 * SUB, LANES), f32),
            sem((3, groups)), sem((groups,)), sem((2, 2)), sem((2, 2, 2)), sem((2, 3, 2)), sem((2, n, 2)),
        ],
        compiler_params=pltpu.CompilerParams(
            collective_id=0, has_side_effects=True, vmem_limit_bytes=60 * 1024 * 1024
        ),
    )(planes(warmth), planes(conductivity), planes(sources))
    return out.reshape(groups, blocks, SUB, LANES).transpose(0, 2, 1, 3).reshape(rows, columns)


def solution(mesh):
    spec = P("tile", "seg")
    return jax.shard_map(
        functools.partial(shards, mesh.shape["seg"], mesh.shape["tile"]),
        mesh=mesh,
        in_specs=(spec, spec, spec),
        out_specs=spec,
        check_vma=False,
    )
```

time: 186 us -> 57.9 us (0.31)
  the two profiles are of different devices: /device:TPU:5 before, /device:TPU:0 now
where the time goes in v1:
time: 57.9 us; the launch traced here: 57.7 us
  Pallas kernels  54.7 us (94%)
  local copies, waits for them, and re-layouts  3.05 us (5%)
    pallas_call x1, Pallas kernels, shards(): pl.pallas_call(functools.partial(kernel, (rows, blocks, n_seg, n_tile)),...  54.7 us
    unnamed x1, local copies, waits for them, and re-layouts  3.05 us

profile of v1, /device:TPU:0, one launch (start us, length us, event | category | flops | bytes accessed | tf_op | source)
XLA Modules:
  0.0 57.7 jit_solution(11652731050433648742)
XLA Ops:
  0.0 54.7 %shard_map.37 = f32[4096,128]{1,0:T(8,128)} custom-call(f32[4096,128]{1,0:T(8,128)} %bitcast.21, f32[4096,128]{1,0:T(8,128)} %bitcast.22, s32[4096,128]{1,0:T(8,128)} %bitcast.23), custom_call_target="tpu_custom_call" | custom-call | tf_op jit(solution)/shard_map/pallas_call | solution.py:378
  54.7 3.0 %copy.5 = f32[32,16384]{1,0:T(8,128)} copy(f32[32,16384]{1,0:T(8,128)} %bitcast.20) | data formatting | bytes 4194304

commit v2 on v1

--- a/solution.py
+++ b/solution.py
@@ -15,11 +15,14 @@
 SUB = 8
 MESH = pl.DeviceIdType.MESH
 
+PAD = 8
+TERMS = 5
+
 
 def kernel(
     sizes, u_hbm, k_hbm, s_hbm, out_hbm,
     u_nat, k_nat, s_nat, o_nat,
-    u_0, u_a, u_b, k_row, s_row, c_e, c_w, c_n, c_s, c_0,
+    u_0, u_a, u_b, k_row, s_row, coef,
     col_out, col_in, corner_in, row_out, row_in,
     load_sem, store_sem, col_sems, corner_sems, first_sems, row_sems,
 ):
@@ -33,9 +36,14 @@
     has_side = (seg > 0, seg < n_seg - 1)
     has_row = (tile > 0, tile < n_tile - 1)
     side_step = (-1, 1)
-    left_at, right_at = SUB - 1, SUB + blocks
-    halo_at = (left_at, right_at)
-    edge_at = (SUB, SUB + blocks - 1)
+    own_at = PAD + SUB
+    halo_at = (PAD, own_at + LANES)
+    edge_at = (own_at, own_at + LANES - SUB)
+    edge_lane = (first_lane, last_lane)
+    edge_id = (0, LANES - 1)
+    parts = LANES // SUB
+    length = LANES + 2 * SUB + 2 * PAD
+    zero = jnp.float32(0.0)
 
     def both(a, b):
         return jnp.logical_and(a, b)
@@ -83,33 +91,33 @@
                         ref[top + d, at, :] = zero_plane
                 return c
 
-            lax.fori_loop(0, tiles + 2, clear, 0)
-
-        @pl.when(jnp.logical_not(has_side[side]))
-        def _(side=side):
-            for r in range(rows + 2 * DEEP):
-                for ref in (u_0, k_row, s_row):
-                    ref[r, halo_at[side]:halo_at[side] + 1, :] = zero_plane[:1]
+            lax.fori_loop(0, length // SUB, clear, 0)
+
+    row_refs = (u_0, k_row, s_row)
+    own = pl.ds(own_at, LANES)
+
+    def neighbour_run(end, side):
+        return jnp.where(edge_lane[side], zero, pltpu.roll(end, (1, LANES - 1)[side], 1))
 
     def relayout(g):
         for which in range(3):
             load(which, g).wait()
 
-        def body(j, c):
-            for r in range(SUB):
-                start = g * span + j * SUB * SUB + r
-                at = pl.ds(SUB + j * SUB, SUB)
-                row = DEEP + g * SUB + r
-                u_0[row, at, :] = u_nat[pl.ds(start, SUB, stride=SUB), :]
-                k_row[row, at, :] = k_nat[pl.ds(start, SUB, stride=SUB), :]
-                s_row[row, at, :] = jnp.where(
-                    s_nat[pl.ds(start, SUB, stride=SUB), :] != 0, jnp.float32(1.0), jnp.float32(0.0)
-                )
+        def body(r, c):
+            at = pl.ds(g * span + r, LANES, stride=SUB)
+            row = DEEP + g * SUB + r
+            for which, ref in enumerate(row_refs):
+                plane = (u_nat, k_nat, s_nat)[which][at, :]
+                if which == 2:
+                    plane = jnp.where(plane != 0, jnp.float32(1.0), zero)
+                plane = plane.T
+                ref[row, own, :] = plane
+                ref[row, halo_at[0]:halo_at[0] + SUB, :] = neighbour_run(plane[-SUB:], 0)
+                ref[row, halo_at[1]:halo_at[1] + SUB, :] = neighbour_run(plane[:SUB], 1)
             return c
 
-        lax.fori_loop(0, tiles, body, 0)
-
-    own = pl.ds(SUB, blocks)
+        lax.fori_loop(0, SUB, body, 0, unroll=2)
+
 
     def first_copy(which, side):
         ref, deep = ((u_0, ROUNDS[0]), (k_row, DEEP), (s_row, DEEP))[which]
@@ -150,7 +158,7 @@
 
     def corner_copy(side, vert):
         return pltpu.make_async_remote_copy(
-            src_ref=col_out.at[side, 0 if vert == 0 else groups - 1],
+            src_ref=col_out.at[side],
             dst_ref=corner_in.at[1 - side, 1 - vert],
             send_sem=corner_sems.at[0, side, vert], recv_sem=corner_sems.at[1, 1 - side, 1 - vert],
             device_id=(seg + side_step[side], tile + side_step[vert]), device_id_type=MESH,
@@ -158,13 +166,13 @@
 
     for g in range(1, groups - 1):
         relayout(g)
-    row_refs = (u_0, k_row, s_row)
     for side in range(2):
-        at = edge_at[side]
-        for g in range(groups):
-            for which, ref in enumerate(row_refs):
-                for r in range(SUB):
-                    col_out[side, g, which * SUB + r:which * SUB + r + 1, :] = ref[DEEP + g * SUB + r, at:at + 1, :]
+        for which, ref in enumerate(row_refs):
+            packed = jnp.zeros((SUB, LANES), jnp.float32)
+            for r in range(rows):
+                end = ref[DEEP + r, edge_at[side]:edge_at[side] + SUB, :]
+                packed = jnp.where(lane == r, pltpu.roll(end, (r - edge_id[side]) % LANES, 1), packed)
+            col_out[side, which * SUB:(which + 1) * SUB, :] = packed
 
         @pl.when(has_side[side])
         def _(side=side):
@@ -175,83 +183,87 @@
             def _(side=side, vert=vert):
                 corner_copy(side, vert).start()
 
+    def unpack(ref, side, packed, pairs):
+        at = slice(halo_at[side], halo_at[side] + SUB)
+        for r, row in pairs:
+            end = pltpu.roll(packed, (edge_id[side] - r) % LANES, 1)
+            ref[row, at, :] = jnp.where(edge_lane[side], end, ref[row, at, :])
+
     for side in range(2):
         @pl.when(has_side[side])
         def _(side=side):
             col_copy(1 - side).wait_recv()
-            at = halo_at[side]
-            for g in range(groups):
-                for which, ref in enumerate(row_refs):
-                    for r in range(SUB):
-                        ref[DEEP + g * SUB + r, at:at + 1, :] = col_in[side, g, which * SUB + r:which * SUB + r + 1, :]
-
-    def east(ref, row, base, here):
-        beyond = ref[row, pl.ds(base + 1, SUB), :]
-        return pltpu.roll(jnp.where(first_lane, beyond, here), LANES - 1, 1)
-
-    def west(ref, row, base, here):
-        beyond = ref[row, pl.ds(base - 1, SUB), :]
-        return pltpu.roll(jnp.where(last_lane, beyond, here), 1, 1)
+            for which, ref in enumerate(row_refs):
+                unpack(ref, side, col_in[side, which * SUB:(which + 1) * SUB, :], [(r, DEEP + r) for r in range(rows)])
 
     half = jnp.float32(0.5 * STEP_SIZE)
 
     def prepare(lo, hi):
         def body(g, c):
-            base = g * SUB + left_at
+            base = pl.multiple_of(g * SUB, SUB) + PAD
             at = pl.ds(base, SUB)
-            column = seg * blocks + base - SUB + sublane
-            inside_col = jnp.logical_and(column >= 0, column < n_seg * blocks)
+            cell = base - own_at + sublane
+            outside = both(both(seg == 0, first_lane), cell < 0)
+            outside = jnp.logical_or(outside, both(both(seg == n_seg - 1, last_lane), cell >= LANES))
             above, here = k_row[DEEP + lo - 1, at, :], k_row[DEEP + lo, at, :]
             for r in range(lo, hi):
-                below = k_row[DEEP + r + 1, at, :]
-                live = jnp.logical_and(inside_col, s_row[DEEP + r, at, :] == 0.0)
+                row = DEEP + r
+                below = k_row[row + 1, at, :]
+                live = both(jnp.logical_not(outside), s_row[row, at, :] == 0.0)
                 if r < 0:
-                    live = jnp.logical_and(live, has_row[0])
+                    live = both(live, has_row[0])
                 if r >= rows:
-                    live = jnp.logical_and(live, has_row[1])
-                weight = jnp.where(live, half, jnp.float32(0.0))
-                ce = weight * (here + east(k_row, DEEP + r, base, here))
-                cw = weight * (here + west(k_row, DEEP + r, base, here))
+                    live = both(live, has_row[1])
+                weight = jnp.where(live, half, zero)
+                cw = weight * (here + k_row[row, pl.ds(base - 1, SUB), :])
+                ce = weight * (here + k_row[row, pl.ds(base + 1, SUB), :])
                 cn = weight * (here + above)
                 cs = weight * (here + below)
-                c_e[DEEP + r, at, :] = ce
-                c_w[DEEP + r, at, :] = cw
-                c_n[DEEP + r, at, :] = cn
-                c_s[DEEP + r, at, :] = cs
-                c_0[DEEP + r, at, :] = 1.0 - ((ce + cw) + (cn + cs))
+                for i, term in enumerate((ce, cw, cn, cs, 1.0 - ((ce + cw) + (cn + cs)))):
+                    coef[row, pl.ds(pl.multiple_of(g * (TERMS * SUB), SUB) + i * SUB, SUB), :] = term
                 above, here = here, below
             return c
 
-        lax.fori_loop(0, tiles + 1, body, 0)
-
-    def advance(step, lo, hi):
+        lax.fori_loop(0, parts + 2, body, 0)
+
+    def advance(step, *ranges):
         src, dst = (u_b, u_a) if step % 2 == 0 else (u_a, u_b)
         src = u_0 if step == 0 else src
         last = step == STEPS - 1
 
         def body(g, c):
-            base = g * SUB + (SUB if last else left_at)
+            base = pl.multiple_of(g * SUB, SUB) + PAD
             at = pl.ds(base, SUB)
-            above, here = src[DEEP + lo - 1, at, :], src[DEEP + lo, at, :]
-            for r in range(lo, hi):
-                below = src[DEEP + r + 1, at, :]
-                row = DEEP + r
-                new = (
-                    (c_0[row, at, :] * here + c_n[row, at, :] * above)
-                    + (c_s[row, at, :] * below + c_e[row, at, :] * east(src, row, base, here))
-                    + c_w[row, at, :] * west(src, row, base, here)
-                )
-                if step == 0:
-                    new = jnp.where(s_row[row, at, :] != 0.0, jnp.float32(1.0), new)
-                if last:
-                    start = (r // SUB) * span + g * SUB * SUB + r % SUB
-                    o_nat[pl.ds(start, SUB, stride=SUB), :] = new
-                else:
+            for lo, hi in ranges:
+                above, here = src[DEEP + lo - 1, at, :], src[DEEP + lo, at, :]
+                for r in range(lo, hi):
+                    row = DEEP + r
+                    below = src[row + 1, at, :]
+                    ce, cw, cn, cs, c0 = (
+                        coef[row, pl.ds(pl.multiple_of(g * (TERMS * SUB), SUB) + i * SUB, SUB), :] for i in range(TERMS)
+                    )
+                    new = (
+                        (c0 * here + cn * above)
+                        + (cs * below + ce * src[row, pl.ds(base + 1, SUB), :])
+                        + cw * src[row, pl.ds(base - 1, SUB), :]
+                    )
+                    if step == 0:
+                        new = jnp.where(s_row[row, at, :] != 0.0, jnp.float32(1.0), new)
                     dst[row, at, :] = new
-                above, here = here, below
+                    above, here = here, below
             return c
 
-        lax.fori_loop(0, tiles if last else tiles + 1, body, 0)
+        lax.fori_loop(1 if last else 0, parts + (1 if last else 2), body, 0)
+
+    def give_back(g):
+        done_ref = u_b if STEPS % 2 == 0 else u_a
+
+        def body(r, c):
+            o_nat[pl.ds(g * span + r, LANES, stride=SUB), :] = done_ref[DEEP + g * SUB + r, own, :].T
+            return c
+
+        lax.fori_loop(0, SUB, body, 0, unroll=2)
+        store(g).start()
 
     def row_copy(which, side):
         d = ROUNDS[which]
@@ -268,7 +280,7 @@
                 dst[dst_row + i, at, :] = src[src_row + i, at, :]
             return c
 
-        lax.fori_loop(0, tiles + 2, body, 0)
+        lax.fori_loop(0, length // SUB, body, 0)
 
     def store(g):
         part = pl.ds(g * span, span)
@@ -287,11 +299,11 @@
                     row_copy(which, side).start()
 
         for j in range(1, d + 1):
-            advance(done + j - 1, j, rows - j)
+            advance(done + j - 1, (j, rows - j))
         if which == len(ROUNDS) - 1:
             for g in range(1, groups - 1):
                 if g * SUB >= d and (g + 1) * SUB <= rows - d:
-                    store(g).start()
+                    give_back(g)
 
         if which == 0:
             for side in range(2):
@@ -301,19 +313,26 @@
                         first_arrival(w, side).wait_recv()
                         first_copy(w, side).wait_send()
 
-            for side in range(2):
-                for vert in range(2):
-                    corner = both(has_side[side], has_row[vert])
-                    at = halo_at[side]
-
-                    @pl.when(corner)
-                    def _(side=side, vert=vert, at=at):
+            for vert in range(2):
+                top = 0 if vert == 0 else DEEP + rows
+
+                @pl.when(has_row[vert])
+                def _(vert=vert, top=top):
+                    for ref in row_refs:
+                        for i in range(DEEP):
+                            for side in range(2):
+                                end = ref[top + i, edge_at[1 - side]:edge_at[1 - side] + SUB, :]
+                                ref[top + i, halo_at[side]:halo_at[side] + SUB, :] = neighbour_run(end, side)
+
+                for side in range(2):
+                    @pl.when(both(has_side[side], has_row[vert]))
+                    def _(side=side, vert=vert, top=top):
                         corner_copy(1 - side, 1 - vert).wait_recv()
                         for w, ref in enumerate(row_refs):
-                            for i in range(DEEP):
-                                from_row = w * SUB + (SUB - DEEP + i if vert == 0 else i)
-                                to_row = i if vert == 0 else DEEP + rows + i
-                                ref[to_row, at:at + 1, :] = corner_in[side, vert, from_row:from_row + 1, :]
+                            packed = corner_in[side, vert, w * SUB:(w + 1) * SUB, :]
+                            pairs = [((rows - DEEP if vert == 0 else 0) + i, top + i) for i in range(DEEP)]
+                            unpack(ref, side, packed, pairs)
+
             prepare(1 - DEEP, 1)
             prepare(rows - 1, rows + DEEP - 1)
         else:
@@ -332,17 +351,20 @@
                             cur[top + i, pl.ds(j * SUB, SUB), :] = zero_plane
                         return c
 
-                    lax.fori_loop(0, tiles + 2, clear, 0)
+                    lax.fori_loop(0, length // SUB, clear, 0)
 
         for j in range(1, d + 1):
             final = done + j == STEPS
-            advance(done + j - 1, 0 if final else j - d, j)
-            advance(done + j - 1, rows - j, rows if final else rows - j + d)
+            advance(
+                done + j - 1,
+                (0 if final else j - d, j),
+                (rows - j, rows if final else rows - j + d),
+            )
         done += d
 
     for g in range(groups):
         if not (g * SUB >= d and (g + 1) * SUB <= rows - d):
-            store(g).start()
+            give_back(g)
     for side in range(2):
         @pl.when(has_side[side])
         def _(side=side):
@@ -371,7 +393,9 @@
 
     flat = rows * blocks
     f32 = jnp.float32
-    plane = (rows + 2 * DEEP, blocks + 2 * SUB, LANES)
+    length = LANES + 2 * SUB + 2 * PAD
+    plane = (rows + 2 * DEEP, length, LANES)
+    assert blocks == LANES
     vmem = pltpu.VMEM
     sem = pltpu.SemaphoreType.DMA
     n = len(ROUNDS)
@@ -382,10 +406,11 @@
         out_specs=pl.BlockSpec(memory_space=pl.ANY),
         scratch_shapes=[
             vmem((flat, LANES), f32), vmem((flat, LANES), f32), vmem((flat, LANES), sources.dtype), vmem((flat, LANES), f32),
-        ] + [vmem(plane, f32)] * 10 + [
-            vmem((2, groups, 3 * SUB, LANES), f32), vmem((2, groups, 3 * SUB, LANES), f32),
+        ] + [vmem(plane, f32)] * 5 + [
+            vmem((rows + 2 * DEEP, (LANES // SUB + 2) * TERMS * SUB, LANES), f32),
+            vmem((2, 3 * SUB, LANES), f32), vmem((2, 3 * SUB, LANES), f32),
             vmem((2, 2, 3 * SUB, LANES), f32),
-            vmem((n, 2, DEEP, blocks + 2 * SUB, LANES), f32), vmem((n, 2, DEEP, blocks + 2 * SUB, LANES), f32),
+            vmem((n, 2, DEEP, length, LANES), f32), vmem((n, 2, DEEP, length, LANES), f32),
             sem((3, groups)), sem((groups,)), sem((2, 2)), sem((2, 2, 2)), sem((2, 3, 2)), sem((2, n, 2)),
         ],
         compiler_params=pltpu.CompilerParams(

time: 57.9 us -> 33.9 us (0.59)
  the two profiles are of different devices: /device:TPU:0 before, /device:TPU:1 now
where the time goes in v2:
time: 33.9 us; the launch traced here: 33.7 us
  Pallas kernels  30.7 us (91%)
  local copies, waits for them, and re-layouts  3.05 us (9%)
    pallas_call x1, Pallas kernels, shards(): pl.pallas_call(functools.partial(kernel, (rows, blocks, n_seg, n_tile)),...  30.7 us
    unnamed x1, local copies, waits for them, and re-layouts  3.05 us

profile of v2, /device:TPU:1, one launch (start us, length us, event | category | flops | bytes accessed | tf_op | source)
XLA Modules:
  0.0 33.7 jit_solution(18140910228422362802)
XLA Ops:
  0.0 30.7 %shard_map.37 = f32[4096,128]{1,0:T(8,128)} custom-call(f32[4096,128]{1,0:T(8,128)} %bitcast.21, f32[4096,128]{1,0:T(8,128)} %bitcast.22, s32[4096,128]{1,0:T(8,128)} %bitcast.23), custom_call_target="tpu_custom_call" | custom-call | tf_op jit(solution)/shard_map/pallas_call | solution.py:402
  30.7 3.0 %copy.5 = f32[32,16384]{1,0:T(8,128)} copy(f32[32,16384]{1,0:T(8,128)} %bitcast.20) | data formatting | bytes 4194304

commit v3 on v2

--- a/solution.py
+++ b/solution.py
@@ -16,12 +16,15 @@
 MESH = pl.DeviceIdType.MESH
 
 PAD = 8
-TERMS = 5
+TERMS = 4
+VMEM_KERNEL = 44 * 1024 * 1024
+VMEM_LAST = 8 * 1024 * 1024
+TERM_ROWS = 5 * SUB
 
 
 def kernel(
     sizes, u_hbm, k_hbm, s_hbm, out_hbm,
-    u_nat, k_nat, s_nat, o_nat,
+    u_nat, k_nat, s_nat,
     u_0, u_a, u_b, k_row, s_row, coef,
     col_out, col_in, corner_in, row_out, row_in,
     load_sem, store_sem, col_sems, corner_sems, first_sems, row_sems,
@@ -116,7 +119,7 @@
                 ref[row, halo_at[1]:halo_at[1] + SUB, :] = neighbour_run(plane[:SUB], 1)
             return c
 
-        lax.fori_loop(0, SUB, body, 0, unroll=2)
+        lax.fori_loop(0, SUB, body, 0, unroll=4)
 
 
     def first_copy(which, side):
@@ -189,16 +192,9 @@
             end = pltpu.roll(packed, (edge_id[side] - r) % LANES, 1)
             ref[row, at, :] = jnp.where(edge_lane[side], end, ref[row, at, :])
 
-    for side in range(2):
-        @pl.when(has_side[side])
-        def _(side=side):
-            col_copy(1 - side).wait_recv()
-            for which, ref in enumerate(row_refs):
-                unpack(ref, side, col_in[side, which * SUB:(which + 1) * SUB, :], [(r, DEEP + r) for r in range(rows)])
-
     half = jnp.float32(0.5 * STEP_SIZE)
 
-    def prepare(lo, hi):
+    def prepare(lo, hi, first=0, end=parts + 2):
         def body(g, c):
             base = pl.multiple_of(g * SUB, SUB) + PAD
             at = pl.ds(base, SUB)
@@ -219,12 +215,12 @@
                 ce = weight * (here + k_row[row, pl.ds(base + 1, SUB), :])
                 cn = weight * (here + above)
                 cs = weight * (here + below)
-                for i, term in enumerate((ce, cw, cn, cs, 1.0 - ((ce + cw) + (cn + cs)))):
-                    coef[row, pl.ds(pl.multiple_of(g * (TERMS * SUB), SUB) + i * SUB, SUB), :] = term
+                for i, term in enumerate((ce, cw, cn, cs)):
+                    coef[row, pl.ds(pl.multiple_of(g * TERM_ROWS, SUB) + i * SUB, SUB), :] = term
                 above, here = here, below
             return c
 
-        lax.fori_loop(0, parts + 2, body, 0)
+        lax.fori_loop(first, end, body, 0)
 
     def advance(step, *ranges):
         src, dst = (u_b, u_a) if step % 2 == 0 else (u_a, u_b)
@@ -235,35 +231,26 @@
             base = pl.multiple_of(g * SUB, SUB) + PAD
             at = pl.ds(base, SUB)
             for lo, hi in ranges:
-                above, here = src[DEEP + lo - 1, at, :], src[DEEP + lo, at, :]
+                here = src[DEEP + lo, at, :]
+                rise = here - src[DEEP + lo - 1, at, :]
                 for r in range(lo, hi):
                     row = DEEP + r
                     below = src[row + 1, at, :]
-                    ce, cw, cn, cs, c0 = (
-                        coef[row, pl.ds(pl.multiple_of(g * (TERMS * SUB), SUB) + i * SUB, SUB), :] for i in range(TERMS)
+                    ce, cw, cn, cs = (
+                        coef[row, pl.ds(pl.multiple_of(g * TERM_ROWS, SUB) + i * SUB, SUB), :] for i in range(TERMS)
                     )
-                    new = (
-                        (c0 * here + cn * above)
-                        + (cs * below + ce * src[row, pl.ds(base + 1, SUB), :])
-                        + cw * src[row, pl.ds(base - 1, SUB), :]
+                    fall = below - here
+                    new = here + (
+                        (cs * fall - cn * rise)
+                        + (ce * (src[row, pl.ds(base + 1, SUB), :] - here) + cw * (src[row, pl.ds(base - 1, SUB), :] - here))
                     )
                     if step == 0:
                         new = jnp.where(s_row[row, at, :] != 0.0, jnp.float32(1.0), new)
                     dst[row, at, :] = new
-                    above, here = here, below
+                    here, rise = below, fall
             return c
 
-        lax.fori_loop(1 if last else 0, parts + (1 if last else 2), body, 0)
-
-    def give_back(g):
-        done_ref = u_b if STEPS % 2 == 0 else u_a
-
-        def body(r, c):
-            o_nat[pl.ds(g * span + r, LANES, stride=SUB), :] = done_ref[DEEP + g * SUB + r, own, :].T
-            return c
-
-        lax.fori_loop(0, SUB, body, 0, unroll=2)
-        store(g).start()
+        lax.fori_loop(1 if last else 0, parts + (1 if last else 2), body, 0, unroll=2 if len(ranges) > 1 else 1)
 
     def row_copy(which, side):
         d = ROUNDS[which]
@@ -283,11 +270,21 @@
         lax.fori_loop(0, length // SUB, body, 0)
 
     def store(g):
-        part = pl.ds(g * span, span)
-        return pltpu.make_async_copy(o_nat.at[part], out_hbm.at[part], store_sem.at[g])
+        done_ref = u_b if STEPS % 2 == 0 else u_a
+        return pltpu.make_async_copy(
+            done_ref.at[pl.ds(DEEP + g * SUB, SUB), own], out_hbm.at[pl.ds(g * SUB, SUB)], store_sem.at[g]
+        )
 
     done = 0
-    prepare(1, rows - 1)
+    prepare(1, rows - 1, 2, parts)
+    for side in range(2):
+        @pl.when(has_side[side])
+        def _(side=side):
+            col_copy(1 - side).wait_recv()
+            for which, ref in enumerate(row_refs):
+                unpack(ref, side, col_in[side, which * SUB:(which + 1) * SUB, :], [(r, DEEP + r) for r in range(rows)])
+    prepare(1, rows - 1, 0, 2)
+    prepare(1, rows - 1, parts, parts + 2)
     for which, d in enumerate(ROUNDS):
         if which:
             cur = u_a if done % 2 == 1 else u_b
@@ -303,7 +300,7 @@
         if which == len(ROUNDS) - 1:
             for g in range(1, groups - 1):
                 if g * SUB >= d and (g + 1) * SUB <= rows - d:
-                    give_back(g)
+                    store(g).start()
 
         if which == 0:
             for side in range(2):
@@ -364,7 +361,7 @@
 
     for g in range(groups):
         if not (g * SUB >= d and (g + 1) * SUB <= rows - d):
-            give_back(g)
+            store(g).start()
     for side in range(2):
         @pl.when(has_side[side])
         def _(side=side):
@@ -381,6 +378,11 @@
                 row_copy(which, side).wait_send()
     for g in range(groups):
         store(g).wait()
+
+
+def give_back(planes, out):
+    for r in range(SUB):
+        out[pl.ds(r, LANES, stride=SUB), :] = planes[r].T
 
 
 def shards(n_seg, n_tile, warmth, conductivity, sources):
@@ -401,22 +403,30 @@
     n = len(ROUNDS)
     out = pl.pallas_call(
         functools.partial(kernel, (rows, blocks, n_seg, n_tile)),
-        out_shape=jax.ShapeDtypeStruct((flat, LANES), f32),
+        out_shape=jax.ShapeDtypeStruct((rows, LANES, LANES), f32),
         in_specs=[pl.BlockSpec(memory_space=pl.ANY)] * 3,
         out_specs=pl.BlockSpec(memory_space=pl.ANY),
         scratch_shapes=[
-            vmem((flat, LANES), f32), vmem((flat, LANES), f32), vmem((flat, LANES), sources.dtype), vmem((flat, LANES), f32),
+            vmem((flat, LANES), f32), vmem((flat, LANES), f32), vmem((flat, LANES), sources.dtype),
         ] + [vmem(plane, f32)] * 5 + [
-            vmem((rows + 2 * DEEP, (LANES // SUB + 2) * TERMS * SUB, LANES), f32),
+            vmem((rows + 2 * DEEP, (LANES // SUB + 2) * TERM_ROWS, LANES), f32),
             vmem((2, 3 * SUB, LANES), f32), vmem((2, 3 * SUB, LANES), f32),
             vmem((2, 2, 3 * SUB, LANES), f32),
             vmem((n, 2, DEEP, length, LANES), f32), vmem((n, 2, DEEP, length, LANES), f32),
             sem((3, groups)), sem((groups,)), sem((2, 2)), sem((2, 2, 2)), sem((2, 3, 2)), sem((2, n, 2)),
         ],
         compiler_params=pltpu.CompilerParams(
-            collective_id=0, has_side_effects=True, vmem_limit_bytes=60 * 1024 * 1024
+            collective_id=0, has_side_effects=True, vmem_limit_bytes=VMEM_KERNEL
         ),
     )(planes(warmth), planes(conductivity), planes(sources))
+    out = pl.pallas_call(
+        give_back,
+        grid=(groups,),
+        out_shape=jax.ShapeDtypeStruct((flat, LANES), f32),
+        in_specs=[pl.BlockSpec((SUB, LANES, LANES), lambda g: (g, 0, 0))],
+        out_specs=pl.BlockSpec((blocks * SUB, LANES), lambda g: (g, 0)),
+        compiler_params=pltpu.CompilerParams(vmem_limit_bytes=VMEM_LAST),
+    )(out)
     return out.reshape(groups, blocks, SUB, LANES).transpose(0, 2, 1, 3).reshape(rows, columns)
 
 

time: 33.9 us -> 32.4 us (0.956)
  Pallas kernels: 30.7 us -> 27.4 us
  local copies, waits for them, and re-layouts: 3.05 us -> 4.77 us
    pallas_call x1, Pallas kernels: 30.7 us -> 25.2 us  [shards(): pl.pallas_call(functools.partial(kernel, (rows, blocks, n_seg, n_tile)),...]
    pallas_call x0 -> x1, Pallas kernels: none -> 2.23 us  [shards(): pl.pallas_call(give_back, grid=(groups,), out_shape=jax.ShapeDtypeStruct(...]
    unnamed x1 -> x6, local copies, waits for them, and re-layouts: 3.05 us -> 4.77 us
where the time goes in v3:
time: 32.4 us; the launch traced here: 32.2 us
  Pallas kernels  27.4 us (85%)
  local copies, waits for them, and re-layouts  4.77 us (15%)
    pallas_call x1, Pallas kernels, shards(): pl.pallas_call(functools.partial(kernel, (rows, blocks, n_seg, n_tile)),...  25.2 us
    unnamed x6, local copies, waits for them, and re-layouts  4.77 us
    pallas_call x1, Pallas kernels, shards(): pl.pallas_call(give_back, grid=(groups,), out_shape=jax.ShapeDtypeStruct(...  2.23 us

profile of v3, /device:TPU:1, one launch (start us, length us, event | category | flops | bytes accessed | tf_op | source)
XLA Modules:
  0.0 32.2 jit_solution(9732293599406836899)
XLA Ops:
  0.0 0.0 copy-start
  0.0 1.6 %copy-done = f32[32,16384]{1,0:T(8,128)S(1)} copy-done((f32[32,16384]{1,0:T(8,128)S(1)}, f32[32,16384]{1,0:T(8,128)}, u32[]{:S(2)}) %copy-start) | copy-done | bytes 2097176
  1.6 0.0 copy-start.1
  1.6 1.6 %copy-done.1 = f32[32,16384]{1,0:T(8,128)S(1)} copy-done((f32[32,16384]{1,0:T(8,128)S(1)}, f32[32,16384]{1,0:T(8,128)}, u32[]{:S(2)}) %copy-start.1) | copy-done | bytes 2097176
  3.2 0.0 copy-start.2
  3.2 1.6 %copy-done.2 = s32[32,16384]{1,0:T(8,128)S(1)} copy-done((s32[32,16384]{1,0:T(8,128)S(1)}, s32[32,16384]{1,0:T(8,128)}, u32[]{:S(2)}) %copy-start.2) | copy-done | bytes 2097176
  4.8 25.2 %shard_map.37.planes = f32[32,128,128]{2,1,0:T(8,128)S(1)} custom-call(f32[4096,128]{1,0:T(8,128)S(1)} %bitcast.20, f32[4096,128]{1,0:T(8,128)S(1)} %bitcast.21, s32[4096,128]{1,0:T(8,128)S(1)} %bitcast.22), custom_call_target="tpu_custom_call" | custom-call | tf_op jit(solution)/shard_map/pallas_call | solution.py:404
  30.0 2.2 %shard_map.38 = f32[4096,128]{1,0:T(8,128)} custom-call(f32[32,128,128]{2,1,0:T(8,128)S(1)} %shard_map.37.planes), custom_call_target="tpu_custom_call" | custom-call | tf_op jit(solution)/shard_map/pallas_call | solution.py:422
Async XLA Ops:
  0.0 1.6 %copy-start = (f32[32,16384]{1,0:T(8,128)S(1)}, f32[32,16384]{1,0:T(8,128)}, u32[]{:S(2)}) copy-start(f32[32,16384]{1,0:T(8,128)} %param.3) | copy-start | bytes 6291460
  1.6 1.6 %copy-start.1 = (f32[32,16384]{1,0:T(8,128)S(1)}, f32[32,16384]{1,0:T(8,128)}, u32[]{:S(2)}) copy-start(f32[32,16384]{1,0:T(8,128)} %param.4) | copy-start | bytes 6291460
  3.2 1.6 %copy-start.2 = (s32[32,16384]{1,0:T(8,128)S(1)}, s32[32,16384]{1,0:T(8,128)}, u32[]{:S(2)}) copy-start(s32[32,16384]{1,0:T(8,128)} %param.5) | copy-start | bytes 6291460

commit v4 on v3

--- a/solution.py
+++ b/solution.py
@@ -15,9 +15,9 @@
 SUB = 8
 MESH = pl.DeviceIdType.MESH
 
-PAD = 8
+PAD = 16
 TERMS = 4
-VMEM_KERNEL = 44 * 1024 * 1024
+VMEM_KERNEL = 50 * 1024 * 1024
 VMEM_LAST = 8 * 1024 * 1024
 TERM_ROWS = 5 * SUB
 
@@ -260,14 +260,13 @@
             device_id=(seg, tile + side_step[side]), device_id_type=MESH,
         )
 
-    def move_rows(src, src_row, dst, dst_row, d):
+    def move_rows(src, src_row, src_at, dst, dst_row, dst_at, d):
         def body(j, c):
-            at = pl.ds(j * SUB, SUB)
             for i in range(d):
-                dst[dst_row + i, at, :] = src[src_row + i, at, :]
+                dst[dst_row + i, pl.ds(dst_at + j * SUB, SUB), :] = src[src_row + i, pl.ds(src_at + j * SUB, SUB), :]
             return c
 
-        lax.fori_loop(0, length // SUB, body, 0)
+        lax.fori_loop(0, parts + 2, body, 0)
 
     def store(g):
         done_ref = u_b if STEPS % 2 == 0 else u_a
@@ -289,7 +288,7 @@
         if which:
             cur = u_a if done % 2 == 1 else u_b
             for side in range(2):
-                move_rows(cur, DEEP if side == 0 else DEEP + rows - d, row_out.at[which, side], 0, d)
+                move_rows(cur, DEEP if side == 0 else DEEP + rows - d, PAD, row_out.at[which, side], 0, 0, d)
 
                 @pl.when(has_row[side])
                 def _(which=which, side=side):
@@ -339,7 +338,7 @@
                 @pl.when(has_row[side])
                 def _(which=which, side=side, top=top, cur=cur, d=d):
                     row_copy(which, 1 - side).wait_recv()
-                    move_rows(row_in.at[which, side], 0, cur, top, d)
+                    move_rows(row_in.at[which, side], 0, 0, cur, top, PAD, d)
 
                 @pl.when(jnp.logical_not(has_row[side]))
                 def _(top=top, cur=cur, d=d):
@@ -404,7 +403,7 @@
     out = pl.pallas_call(
         functools.partial(kernel, (rows, blocks, n_seg, n_tile)),
         out_shape=jax.ShapeDtypeStruct((rows, LANES, LANES), f32),
-        in_specs=[pl.BlockSpec(memory_space=pl.ANY)] * 3,
+        in_specs=[pl.BlockSpec(memory_space=pltpu.HBM)] * 3,
         out_specs=pl.BlockSpec(memory_space=pl.ANY),
         scratch_shapes=[
             vmem((flat, LANES), f32), vmem((flat, LANES), f32), vmem((flat, LANES), sources.dtype),
@@ -412,7 +411,7 @@
             vmem((rows + 2 * DEEP, (LANES // SUB + 2) * TERM_ROWS, LANES), f32),
             vmem((2, 3 * SUB, LANES), f32), vmem((2, 3 * SUB, LANES), f32),
             vmem((2, 2, 3 * SUB, LANES), f32),
-            vmem((n, 2, DEEP, length, LANES), f32), vmem((n, 2, DEEP, length, LANES), f32),
+            vmem((n, 2, DEEP, LANES + 2 * SUB, LANES), f32), vmem((n, 2, DEEP, LANES + 2 * SUB, LANES), f32),
             sem((3, groups)), sem((groups,)), sem((2, 2)), sem((2, 2, 2)), sem((2, 3, 2)), sem((2, n, 2)),
         ],
         compiler_params=pltpu.CompilerParams(

time: 32.4 us -> 26.9 us (0.83)
  local copies, waits for them, and re-layouts: 4.77 us -> 0 us
  Pallas kernels: 27.4 us -> 26.8 us
    unnamed x6 -> x0, local copies, waits for them, and re-layouts: 4.77 us -> none
    pallas_call x1, Pallas kernels: 25.2 us -> 24.5 us  [shards(): pl.pallas_call(functools.partial(kernel, (rows, blocks, n_seg, n_tile)),...]
where the time goes in v4:
time: 26.9 us; the launch traced here: 26.8 us
  Pallas kernels  26.8 us (100%)
    pallas_call x1, Pallas kernels, shards(): pl.pallas_call(functools.partial(kernel, (rows, blocks, n_seg, n_tile)),...  24.5 us
    pallas_call x1, Pallas kernels, shards(): pl.pallas_call(give_back, grid=(groups,), out_shape=jax.ShapeDtypeStruct(...  2.23 us

profile of v4, /device:TPU:1, one launch (start us, length us, event | category | flops | bytes accessed | tf_op | source)
XLA Modules:
  0.0 26.8 jit_solution(7521366649575028507)
XLA Ops:
  0.0 24.5 %shard_map.37.planes = f32[32,128,128]{2,1,0:T(8,128)S(1)} custom-call(f32[4096,128]{1,0:T(8,128)} %bitcast.20, f32[4096,128]{1,0:T(8,128)} %bitcast.21, s32[4096,128]{1,0:T(8,128)} %bitcast.22), custom_call_target="tpu_custom_call" | custom-call | tf_op jit(solution)/shard_map/pallas_call | solution.py:403
  24.5 2.2 %shard_map.38 = f32[4096,128]{1,0:T(8,128)} custom-call(f32[32,128,128]{2,1,0:T(8,128)S(1)} %shard_map.37.planes), custom_call_target="tpu_custom_call" | custom-call | tf_op jit(solution)/shard_map/pallas_call | solution.py:421
